TPU v7x, 32 devices: a whole 2x2x4 slice. The times are simulated.
32 devices in a mesh: dp: 4 (over x, y), tp: 8 (over z, core).
Axes of the slice: x: 2, y: 2, z: 4, core: 2. Of those that a mesh axis runs over, the one named last changes fastest.
Arguments:
- x_tokens: bfloat16 [4, 2048, 2560], P('dp', 'tp'), parts along dimension 0
- ln1_gain: float32 [2, 2560], replicated
- ln1_bias: float32 [2, 2560], replicated
- ln2_gain: float32 [2, 2560], replicated
- ln2_bias: float32 [2, 2560], replicated
- w_qkv: bfloat16 [2, 2560, 3, 32, 80], P(None, None, None, 'tp')
- w_out: bfloat16 [2, 32, 80, 2560], P(None, 'tp')
- b_out: float32 [2, 2560], replicated
- w_up: bfloat16 [2, 2560, 10240], P(None, None, 'tp')
- b_up: float32 [2, 10240], P(None, 'tp')
- w_down: bfloat16 [2, 10240, 2560], P(None, 'tp')
- b_down: float32 [2, 2560], replicated
Outputs:
- output: bfloat16 [4, 2048, 2560], P('dp', 'tp'), parts along dimension 0
There are 4 independent parts. A program takes and returns all parts, laid end to end along the dimension named above; an argument that names none is the same for every part.
All inputs are finite; a program needn't handle non-finite values.
Results may differ from a plain program's by a relative error of at most 0.0104064.
Values are sent between devices in bfloat16 or wider.
A program may use at most 1 GiB of HBM per device.

v0:
```python
import math
import jax
import jax.numpy as jnp
from jax import lax
from jax.sharding import PartitionSpec as P


def layer_norm(resid, gain, shift):
    row_mean = jnp.mean(resid, axis=-1, keepdims=True)
    centered = resid - row_mean
    variance = jnp.mean(centered * centered, axis=-1, keepdims=True)
    return (centered * lax.rsqrt(variance + 1e-5) * gain + shift).astype(jnp.bfloat16)


def solution(mesh):
    tp_size = mesh.shape["tp"]

    def scatter_rows(partial):
        batch, seq_len, width = partial.shape
        pieces = partial.astype(jnp.bfloat16).reshape(batch, tp_size, seq_len // tp_size, width)
        received = lax.all_to_all(pieces, "tp", 1, 1, tiled=True)
        return jnp.sum(received.astype(jnp.float32), axis=1)

    def local_forward(x_local, ln1_gain, ln1_bias, ln2_gain, ln2_bias, w_qkv, w_out, b_out, w_up, b_up, w_down, b_down):
        seq_len = x_local.shape[1] * tp_size
        scale = 1.0 / math.sqrt(w_out.shape[2])
        positions = jnp.arange(seq_len)
        causal = positions[:, None] >= positions[None, :]
        resid = x_local.astype(jnp.float32)
        for layer in range(w_qkv.shape[0]):
            normed = layer_norm(resid, ln1_gain[layer], ln1_bias[layer])
            gathered = lax.all_gather(normed, "tp", axis=1, tiled=True)
            qkv_proj = jnp.einsum("bsd,dthe->tbhse", gathered, w_qkv[layer], preferred_element_type=jnp.float32).astype(jnp.bfloat16)
            scores = jnp.einsum("bhqe,bhke->bhqk", qkv_proj[0], qkv_proj[1], preferred_element_type=jnp.float32) * scale
            attn_probs = jax.nn.softmax(jnp.where(causal, scores, -1e30), axis=-1).astype(jnp.bfloat16)
            attn_heads = jnp.einsum("bhqk,bhke->bhqe", attn_probs, qkv_proj[2], preferred_element_type=jnp.float32).astype(jnp.bfloat16)
            partial = jnp.einsum("cirf,ife->cre", attn_heads, w_out[layer], preferred_element_type=jnp.float32)
            resid = resid + (scatter_rows(partial) + b_out[layer])
            normed_mlp = layer_norm(resid, ln2_gain[layer], ln2_bias[layer])
            gathered_mlp = lax.all_gather(normed_mlp, "tp", axis=1, tiled=True)
            pre_act = jnp.einsum("bsd,df->bsf", gathered_mlp, w_up[layer], preferred_element_type=jnp.float32) + b_up[layer]
            hidden = jax.nn.gelu(pre_act, approximate=True).astype(jnp.bfloat16)
            partial_mlp = jnp.einsum("bsf,fd->bsd", hidden, w_down[layer], preferred_element_type=jnp.float32)
            resid = resid + (scatter_rows(partial_mlp) + b_down[layer])
        return resid.astype(jnp.bfloat16)

    rows_spec = P("dp", "tp", None)
    in_specs = (rows_spec, P(), P(), P(), P(), P(None, None, None, "tp", None), P(None, "tp", None, None), P(), P(None, None, "tp"), P(None, "tp"), P(None, "tp", None), P())
    return jax.shard_map(local_forward, mesh=mesh, in_specs=in_specs, out_specs=rows_spec, check_vma=False)
```

profile of v0, /device:TPU:0, one launch (start us, length us, event | category | flops | bytes accessed | tf_op | source)
XLA Modules:
  0.0 1627.9 jit_solution(10620468945458689300)
XLA Ops:
  18.6 8.5 fusion.105
  27.0 89.2 %all-gather.5.cloned.1.call-done = bf16[1,2048,2560]{2,1,0:T(8,128)(2,1)} async-done(((bf16[1,256,2560]{2,1,0:T(8,128)(2,1)}), bf16[1,2048,2560]{2,1,0:T(8,128)(2,1)}) %all-gather.5.cloned.1.call-update) | async-done | bytes 10485776 | tf_op jit(solution)/shard_map/all_gather | solution.py:32
  116.2 15.0 fusion.34
  133.8 36.4 %fusion.106 = (f32[4,2048]{1,0:T(4,128)S(1)}, f32[4,2048,2048]{1,2,0:T(8,128)}) fusion(pred[2048,2048]{0,1:T(8,128)(4,1)} %iota_compare_fusion, bf16[3,1,4,2048,80]{3,4,2,0,1:T(8,128)(2,1)} %convert_bitcast_fusion.1), kind=kOutput, calls=%fused_computation.150 | convolution fusion | flops 2751465472 | bytes 73957376 | tf_op jit(solution)/shard_map/sub | solution.py:35
  170.2 28.4 %bitcast_convert_fusion.1 = bf16[2048,2560]{1,0:T(8,128)(2,1)} fusion(bf16[2,4,80,2560]{3,2,1,0:T(8,128)(2,1)S(1)} %copy-done.16, f32[4,2048,2048]{1,2,0:T(8,128)} %get-tuple-element.26, f32[4,2048]{1,0:T(4,128)S(1)} %get-tuple-element.25, bf16[3,1,4,2048,80]{3,4,2,0,1:T(8,128)(2,1)} %convert_bitcast_fusion.1), kind=kOutput, calls=%fused_computation.19 | convolution fusion | flops 6079250432 | bytes 80576512 | tf_op jit(solution)/shard_map/cirf,ife->cre/dot_general | solution.py:37
  198.7 5.3 all-to-all-start
  205.4 227.1 %all-to-all-done = bf16[1,8,256,2560]{3,2,0,1:T(8,128)(2,1)} async-done(((bf16[1,8,256,2560]{3,2,0,1:T(8,128)(2,1)}), bf16[1,8,256,2560]{3,2,0,1:T(8,128)(2,1)}, u32[]{:S(2)}, u32[]{:S(2)}) %all-to-all-start) | async-done | bytes 10485792 | tf_op jit(solution)/shard_map/all_to_all | solution.py:21
  432.4 5.8 convert_reduce_fusion.3
  442.0 97.1 %all-gather.7.cloned.1.call-done = bf16[1,2048,2560]{2,1,0:T(8,128)(2,1)} async-done(((bf16[1,256,2560]{2,1,0:T(8,128)(2,1)}), bf16[1,2048,2560]{2,1,0:T(8,128)(2,1)}) %all-gather.7.cloned.1.call-update) | async-done | bytes 10485776 | tf_op jit(solution)/shard_map/all_gather | solution.py:40
  539.1 19.5 %fusion.19.clone.5 = bf16[2048,1280]{1,0:T(8,128)(2,1)S(1)} fusion(bf16[1,2048,2560]{2,1,0:T(8,128)(2,1)} %all-gather.7.cloned.1.call-done, bf16[2,2560,1280]{2,1,0:T(8,128)(2,1)} %param.20, f32[1280]{0:T(1024)S(1)} %get-tuple-element.18), kind=kOutput, calls=%fused_computation.36.clone.clone.clone.2 | convolution fusion | flops 13447987200 | bytes 22287360 | tf_op jit(solution)/shard_map/bsd,df->bsf/dot_general | solution.py:41
  558.6 18.6 %convolution_convert_fusion.1 = bf16[2048,2560]{1,0:T(8,128)(2,1)} fusion(bf16[2,1280,2560]{2,1,0:T(8,128)(2,1)} %param.22, bf16[2048,1280]{1,0:T(8,128)(2,1)S(1)} %fusion.19.clone.5), kind=kOutput, calls=%fused_computation.28 | convolution fusion | flops 13427015680 | bytes 22282240 | tf_op jit(solution)/shard_map/bsf,fd->bsd/dot_general | solution.py:43
  583.4 227.6 %all-to-all-done.1 = bf16[1,8,256,2560]{3,2,0,1:T(8,128)(2,1)} async-done(((bf16[1,8,256,2560]{3,2,0,1:T(8,128)(2,1)}), bf16[1,8,256,2560]{3,2,0,1:T(8,128)(2,1)}, u32[]{:S(2)}, u32[]{:S(2)}) %all-to-all-start.1) | async-done | bytes 10485792 | tf_op jit(solution)/shard_map/all_to_all | solution.py:21
  811.0 5.9 convert_reduce_fusion.2
  821.1 97.7 %all-gather.9.cloned.1.call-done = bf16[1,2048,2560]{2,1,0:T(8,128)(2,1)} async-done(((bf16[1,256,2560]{2,1,0:T(8,128)(2,1)}), bf16[1,2048,2560]{2,1,0:T(8,128)(2,1)}) %all-gather.9.cloned.1.call-update) | async-done | bytes 10485776 | tf_op jit(solution)/shard_map/all_gather | solution.py:32
  918.8 14.5 fusion.30
  936.0 36.4 %fusion.107 = (f32[4,2048]{1,0:T(4,128)S(1)}, f32[4,2048,2048]{1,2,0:T(8,128)}) fusion(pred[2048,2048]{0,1:T(8,128)(4,1)} %iota_compare_fusion, bf16[3,1,4,2048,80]{3,4,2,0,1:T(8,128)(2,1)} %convert_bitcast_fusion), kind=kOutput, calls=%fused_computation.151 | convolution fusion | flops 2751465472 | bytes 73957376 | tf_op jit(solution)/shard_map/sub | solution.py:35
  972.4 28.7 %bitcast_convert_fusion = bf16[2048,2560]{1,0:T(8,128)(2,1)} fusion(bf16[2,4,80,2560]{3,2,1,0:T(8,128)(2,1)S(1)} %copy-done.17, f32[4,2048,2048]{1,2,0:T(8,128)} %get-tuple-element.28, f32[4,2048]{1,0:T(4,128)S(1)} %get-tuple-element.27, bf16[3,1,4,2048,80]{3,4,2,0,1:T(8,128)(2,1)} %convert_bitcast_fusion), kind=kOutput, calls=%fused_computation.18 | convolution fusion | flops 6079250432 | bytes 80576512 | tf_op jit(solution)/shard_map/cirf,ife->cre/dot_general | solution.py:37
  1001.0 234.9 %all_to_all.20 = bf16[1,8,256,2560]{3,2,0,1:T(8,128)(2,1)} all-to-all(bf16[1,8,256,2560]{3,2,0,1:T(8,128)(2,1)} %bitcast.187), channel_id=1, replica_groups=mesh['dp'=4,'tp'=8] {'tp'}, dimensions={1} | all-to-all | bytes 20971520 | tf_op jit(solution)/shard_map/all_to_all | solution.py:21
  1235.9 6.0 convert_reduce_fusion.1
  1244.4 100.4 %all-gather.11.cloned.1.call-done = bf16[1,2048,2560]{2,1,0:T(8,128)(2,1)} async-done(((bf16[1,256,2560]{2,1,0:T(8,128)(2,1)}), bf16[1,2048,2560]{2,1,0:T(8,128)(2,1)}) %all-gather.11.cloned.1.call-update) | async-done | bytes 10485776 | tf_op jit(solution)/shard_map/all_gather | solution.py:40
  1344.8 19.5 %fusion.27.clone.5 = bf16[2048,1280]{1,0:T(8,128)(2,1)S(1)} fusion(bf16[1,2048,2560]{2,1,0:T(8,128)(2,1)} %all-gather.11.cloned.1.call-done, bf16[2,2560,1280]{2,1,0:T(8,128)(2,1)} %param.20, f32[1280]{0:T(1024)S(1)} %copy-done.15), kind=kOutput, calls=%fused_computation.44.clone.clone.clone.2 | convolution fusion | flops 13447987200 | bytes 22287360 | tf_op jit(solution)/shard_map/bsd,df->bsf/dot_general | solution.py:41
  1364.3 17.0 %convolution_convert_fusion = bf16[2048,2560]{1,0:T(8,128)(2,1)S(1)} fusion(bf16[2,1280,2560]{2,1,0:T(8,128)(2,1)} %param.22, bf16[2048,1280]{1,0:T(8,128)(2,1)S(1)} %fusion.27.clone.5), kind=kOutput, calls=%fused_computation.27 | convolution fusion | flops 13427015680 | bytes 22282240 | tf_op jit(solution)/shard_map/bsf,fd->bsd/dot_general | solution.py:43
  1381.3 232.5 %all_to_all.21 = bf16[1,8,256,2560]{3,2,0,1:T(8,128)(2,1)} all-to-all(bf16[1,8,256,2560]{3,2,0,1:T(8,128)(2,1)S(1)} %bitcast.188), channel_id=1, replica_groups=mesh['dp'=4,'tp'=8] {'tp'}, dimensions={1} | all-to-all | bytes 20971520 | tf_op jit(solution)/shard_map/all_to_all | solution.py:21
  1613.8 5.8 convert_reduce_fusion
  (74 shorter events, 36.7 us)
Async XLA Ops:
  6.5 109.7 %all-gather.5.cloned.1.call-start = ((), (), s32[]{:S(2)}) async-start(), calls=%async_computation.4 | async-start | bytes 11796480 | tf_op jit(solution)/shard_map/all_gather | solution.py:32
  133.8 36.4 %copy-start.16 = (bf16[2,4,80,2560]{3,2,1,0:T(8,128)(2,1)S(1)}, bf16[2,4,80,2560]{3,2,1,0:T(8,128)(2,1)}, u32[]{:S(2)}) copy-start(bf16[2,4,80,2560]{3,2,1,0:T(8,128)(2,1)} %param.18) | copy-start | bytes 9830404
  198.7 5.4 copy-start.10
  198.7 6.0 copy-start.12
  198.7 6.0 copy-start.13
  198.7 233.8 %all-to-all-start = ((bf16[1,8,256,2560]{3,2,0,1:T(8,128)(2,1)}), bf16[1,8,256,2560]{3,2,0,1:T(8,128)(2,1)}, u32[]{:S(2)}, u32[]{:S(2)}) async-start(bf16[1,8,256,2560]{3,2,0,1:T(8,128)(2,1)} %bitcast.185), calls=%async_computation | async-start | bytes 20971520 | tf_op jit(solution)/shard_map/all_to_all | solution.py:21
  204.0 335.2 %all-gather.7.cloned.1.call-start = ((), (), s32[]{:S(2)}) async-start(), calls=%async_computation.5 | async-start | bytes 11796480 | tf_op jit(solution)/shard_map/all_gather | solution.py:40
  432.4 5.8 copy-start
  439.4 2.0 copy-start.14
  577.2 5.5 copy-start.11
  577.2 233.8 %all-to-all-start.1 = ((bf16[1,8,256,2560]{3,2,0,1:T(8,128)(2,1)}), bf16[1,8,256,2560]{3,2,0,1:T(8,128)(2,1)}, u32[]{:S(2)}, u32[]{:S(2)}) async-start(bf16[1,8,256,2560]{3,2,0,1:T(8,128)(2,1)} %bitcast.186), calls=%async_computation.1 | async-start | bytes 20971520 | tf_op jit(solution)/shard_map/all_to_all | solution.py:21
  582.5 336.3 %all-gather.9.cloned.1.call-start = ((), (), s32[]{:S(2)}) async-start(), calls=%async_computation.6 | async-start | bytes 11796480 | tf_op jit(solution)/shard_map/all_gather | solution.py:32
  811.0 5.9 copy-start.1
  816.9 2.5 copy-start.7
  816.9 2.5 copy-start.8
  817.8 1.6 copy-start.2
  821.0 523.8 %all-gather.11.cloned.1.call-start = ((), (), s32[]{:S(2)}) async-start(), calls=%async_computation.7 | async-start | bytes 11796480 | tf_op jit(solution)/shard_map/all_gather | solution.py:40
  935.9 36.4 %copy-start.17 = (bf16[2,4,80,2560]{3,2,1,0:T(8,128)(2,1)S(1)}, bf16[2,4,80,2560]{3,2,1,0:T(8,128)(2,1)}, u32[]{:S(2)}) copy-start(bf16[2,4,80,2560]{3,2,1,0:T(8,128)(2,1)} %param.18) | copy-start | bytes 9830404
  1235.9 6.0 copy-start.3
  1235.9 6.0 copy-start.4
  1241.9 0.8 copy-start.5
  1241.9 0.8 copy-start.6
  1242.3 102.5 %copy-start.15 = (f32[1280]{0:T(1024)S(1)}, f32[1280]{0:T(1024)}, u32[]{:S(2)}) copy-start(f32[1280]{0:T(1024)} %get-tuple-element.17) | copy-start | bytes 15364
  1613.8 5.8 copy-start.9
Sparse Core Ops, SparseCore 0:
  14.5 101.6 all-gather.4
  441.5 97.5 all-gather.6
  821.1 97.5 all-gather.8
  1244.5 100.2 all-gather.10
where the time goes:
time: 1630 us
  waiting for transfers between devices  839 us (51%)
  blocking collectives  467 us (29%)
  matrix products  234 us (14%)
  other arithmetic  49.2 us (3%)
    all_to_all x2, blocking collectives, scatter_rows(): received = lax.all_to_all(pieces, 'tp', 1, 1, tiled=True)  467 us
    all_to_all x2, waiting for transfers between devices, scatter_rows(): received = lax.all_to_all(pieces, 'tp', 1, 1, tiled=True)  455 us
    all_gather x2, waiting for transfers between devices, local_forward(): gathered_mlp = lax.all_gather(normed_mlp, 'tp', axis=1, tiled=True)  198 us
    all_gather x2, waiting for transfers between devices, local_forward(): gathered = lax.all_gather(normed, 'tp', axis=1, tiled=True)  187 us
    sub x2, matrix products, local_forward(): jax.nn.softmax(jnp.where(causal, scores, -1e+30), axis=-1)  72.8 us
    dot_general x2, matrix products, local_forward(): jnp.einsum('cirf,ife->cre', attn_heads, w_out[layer], preferred_element_t...  57.1 us
    dot_general x2, matrix products, local_forward(): jnp.einsum('bsd,df->bsf', gathered_mlp, w_up[layer], preferred_element_ty...  39 us
    dot_general x2, matrix products, local_forward(): jnp.einsum('bsf,fd->bsd', hidden, w_down[layer], preferred_element_type=j...  35.6 us
  transfers between devices with their start and end apart: 6, of which 6 were waited for; matrix products, arithmetic and copies ran while one was open for 1% of the time, Pallas kernels for 0%

commit v1 on v0

v1 whole, which is shorter than its diff:
```python
import functools
import math
import jax
import jax.numpy as jnp
from jax import lax
from jax.experimental import pallas as pl
from jax.experimental.pallas import tpu as pltpu
from jax.sharding import PartitionSpec as P

F32 = jnp.float32
BF16 = jnp.bfloat16
LANES = 128
CHUNK = 32
AHEAD = 2
MESH = pl.DeviceIdType.MESH


def layer_norm(resid, gain, shift):
    row_mean = jnp.mean(resid, axis=-1, keepdims=True)
    centered = resid - row_mean
    variance = jnp.mean(centered * centered, axis=-1, keepdims=True)
    return (centered * lax.rsqrt(variance + 1e-5) * gain + shift).astype(BF16)


def col_tiles(width, tile=512):
    return [(start, min(tile, width - start)) for start in range(0, width, tile)]


def chunk_place(j, chips, per_core):
    turn = (j // 2) % chips
    owner = jnp.where(turn % 2 == 0, turn // 2, chips - 1 - turn // 2)
    return owner, (j // (2 * chips)) * 2 + j % 2


def exchange_kernel(chips, per_core, act, final, *refs):
    if final:
        (x_ref, w_ref, resid_ref, bias_ref, out_ref, part, other, inc, inc2, acc_ref,
         part_s, part_r, sum_s, inc_r, inc2_r) = refs
    else:
        (x_ref, w_ref, resid_ref, bias_ref, gain_ref, shift_ref, w2_ref, b2_ref, out_ref, resid_out, part, other, inc, inc2,
         acc_ref, normed, part_s, part_r, sum_s, inc_r, inc2_r, norm_r, left_s, right_s, mate_s, mate_r) = refs
    n_chunks = chips * per_core
    far = chips - 1
    group = lax.axis_index("dp")
    me = lax.axis_index("tp")
    z, core = me // 2, me % 2
    mate = (group, z * 2 + (1 - core))
    left = (group, jnp.maximum(me - 2, 0))
    right = (group, jnp.minimum(me + 2, 2 * chips - 1))
    has_left, has_right = z > 0, z < far

    def remote(src, dst, send, recv, device):
        return pltpu.make_async_remote_copy(src_ref=src, dst_ref=dst, send_sem=send, recv_sem=recv, device_id=device, device_id_type=MESH)

    barrier = pltpu.get_barrier_semaphore()
    pl.semaphore_signal(barrier, inc=1, device_id=mate, device_id_type=MESH)

    @pl.when(has_left)
    def _():
        pl.semaphore_signal(barrier, inc=1, device_id=left, device_id_type=MESH)

    @pl.when(has_right)
    def _():
        pl.semaphore_signal(barrier, inc=1, device_id=right, device_id_type=MESH)

    pl.semaphore_wait(barrier, 1 + has_left.astype(jnp.int32) + has_right.astype(jnp.int32))

    def matmul_in(j):
        owner, place = chunk_place(j, chips, per_core)
        rows = x_ref[owner, :, pl.ds(place, 2)].reshape(4 * CHUNK, x_ref.shape[-1])
        for start, width in col_tiles(w_ref.shape[1]):
            tile = jnp.dot(rows, w_ref[:, start : start + width], preferred_element_type=F32)
            part[owner, :, pl.ds(place, 2), :, start : start + width] = tile.astype(BF16).reshape(2, 2, CHUNK, width)
        for half in range(2):
            remote(part.at[owner, 1 - core, place + half], other.at[owner, place + half], part_s.at[j + half], part_r.at[j + half], mate).start()

    def own_sum(j, owner, place):
        mine = part.at[owner, core, place]
        remote(mine, other.at[owner, place], part_s.at[j], part_r.at[j], mate).wait_recv()
        acc_ref[...] = mine[...].astype(F32) + other[owner, place].astype(F32)

    def add_inc(j, owner, place):
        remote(inc.at[owner, place], inc.at[owner, place], sum_s.at[j], inc_r.at[j], left).wait_recv()
        acc_ref[...] += inc[owner, place].astype(F32)

    def pass_sum(j, owner, place):
        own_sum(j, owner, place)

        @pl.when(jnp.where(z < owner, has_left, has_right))
        def _():
            add_inc(j, owner, place)

        mine = part.at[owner, core, place]
        mine[...] = acc_ref[...].astype(BF16)

        @pl.when(z < owner)
        def _():
            remote(mine, inc.at[owner, place], sum_s.at[j], inc_r.at[j], right).start()

        @pl.when(z > owner + 1)
        def _():
            remote(mine, inc.at[owner, place], sum_s.at[j], inc_r.at[j], left).start()

        @pl.when(z == owner + 1)
        def _():
            remote(mine, inc2.at[place], sum_s.at[j], inc2_r.at[j], left).start()

    def send_left(j, rows):
        remote(rows, rows, left_s.at[j], norm_r.at[j], left).start()

    def send_right(j, rows):
        remote(rows, rows, right_s.at[j], norm_r.at[j], right).start()

    def finish_sum(j, owner, place):
        own_sum(j, owner, place)

        @pl.when(has_left)
        def _():
            add_inc(j, owner, place)

        @pl.when(has_right)
        def _():
            remote(inc2.at[place], inc2.at[place], sum_s.at[j], inc2_r.at[j], right).wait_recv()
            acc_ref[...] += inc2[place].astype(F32)

        resid = resid_ref[place] + (acc_ref[...] + bias_ref[...])
        if final:
            out_ref[place] = resid.astype(BF16)
            return
        resid_out[place] = resid
        rows = normed.at[owner, core, place]
        rows[...] = layer_norm(resid, gain_ref[...], shift_ref[...])
        pl.when(has_left)(lambda: send_left(j, rows))
        pl.when(has_right)(lambda: send_right(j, rows))
        remote(rows, rows, mate_s.at[j], mate_r.at[j], mate).start()

    def pass_norm(j, owner, place):
        rows = normed.at[owner, core, place]
        remote(rows, rows, left_s.at[j], norm_r.at[j], left).wait_recv()
        pl.when((z < owner) & has_left)(lambda: send_left(j, rows))
        pl.when((z > owner) & has_right)(lambda: send_right(j, rows))
        remote(rows, rows, mate_s.at[j], mate_r.at[j], mate).start()

    def matmul_out(j):
        owner, place = chunk_place(j, chips, per_core)
        for half in range(2):
            rows = normed.at[owner, 1 - core, place + half]
            remote(rows, rows, mate_s.at[j + half], mate_r.at[j + half], mate).wait_recv()
        rows = normed[owner, :, pl.ds(place, 2)].reshape(4 * CHUNK, normed.shape[-1])
        for start, width in col_tiles(w2_ref.shape[1]):
            tile = jnp.dot(rows, w2_ref[:, start : start + width], preferred_element_type=F32)
            if act:
                tile = jax.nn.gelu(tile + b2_ref[:, start : start + width], approximate=True)
            out_ref[owner, :, pl.ds(place, 2), :, start : start + width] = tile.astype(BF16).reshape(2, 2, CHUNK, width)

    def at_distance(j, distance, step):
        inside = (j >= 0) & (j < n_chunks)
        safe = jnp.clip(j, 0, n_chunks - 1)
        owner, place = chunk_place(safe, chips, per_core)
        pl.when(inside & (jnp.abs(z - owner) == distance))(lambda: step(safe, owner, place))

    def tick(t, carry):
        for distance in range(far, -1, -1):
            at_distance(t - AHEAD - far + distance, distance, finish_sum if distance == 0 else pass_sum)
        if not final:
            for distance in range(1, chips):
                at_distance(t - AHEAD - far - distance, distance, pass_norm)

        @pl.when((t % 2 == 0) & (t < n_chunks))
        def _():
            matmul_in(jnp.clip(t, 0, n_chunks - 2))

        if not final:
            late = t - AHEAD - 2 * far - 2

            @pl.when((t % 2 == 0) & (late >= 0))
            def _():
                matmul_out(jnp.clip(late, 0, n_chunks - 2))

        return carry

    ticks = n_chunks + AHEAD + far if final else n_chunks + AHEAD + 2 * far + 1
    lax.fori_loop(0, ticks, tick, 0)

    def drain(j, carry):
        owner, place = chunk_place(j, chips, per_core)
        mine = part.at[owner, core, place]
        remote(mine, other.at[owner, place], part_s.at[j], part_r.at[j], mate).wait_send()

        @pl.when(z != owner)
        def _():
            remote(mine, inc.at[owner, place], sum_s.at[j], inc_r.at[j], left).wait_send()

        if not final:
            rows = normed.at[owner, core, place]

            @pl.when((z <= owner) & has_left)
            def _():
                remote(rows, rows, left_s.at[j], norm_r.at[j], left).wait_send()

            @pl.when((z >= owner) & has_right)
            def _():
                remote(rows, rows, right_s.at[j], norm_r.at[j], right).wait_send()

            remote(rows, rows, mate_s.at[j], mate_r.at[j], mate).wait_send()
        return carry

    lax.fori_loop(0, n_chunks, drain, 0)


def exchange(chips, call_id, x, w, resid, bias, norm=None, w2=None, b2=None):
    seq_len, depth = x.shape
    width = w.shape[1]
    own = resid.shape[0]
    per_core = own // CHUNK
    n_chunks = chips * per_core
    final = norm is None
    blocks = (chips, 2, per_core, CHUNK)
    operands = [x.reshape(*blocks, depth), w, resid.reshape(per_core, CHUNK, width), bias[None]]
    scratch = [
        pltpu.VMEM((*blocks, width), BF16),
        pltpu.VMEM((chips, per_core, CHUNK, width), BF16),
        pltpu.VMEM((chips, per_core, CHUNK, width), BF16),
        pltpu.VMEM((per_core, CHUNK, width), BF16),
        pltpu.VMEM((CHUNK, width), F32),
    ]
    sems = [pltpu.SemaphoreType.DMA((n_chunks,))]
    flops = 2 * seq_len * depth * width
    if final:
        out_shape = jax.ShapeDtypeStruct((per_core, CHUNK, width), BF16)
        scratch += sems * 5
    else:
        width2 = w2.shape[1]
        operands += [norm[0][None], norm[1][None], w2, jnp.zeros((1, width2), F32) if b2 is None else b2[None]]
        out_shape = (jax.ShapeDtypeStruct((*blocks, width2), BF16), jax.ShapeDtypeStruct((per_core, CHUNK, width), F32))
        scratch += [pltpu.VMEM((*blocks, width), BF16)] + sems * 10
        flops += 2 * seq_len * width * width2
    vmem = pl.BlockSpec(memory_space=pltpu.VMEM)
    result = pl.pallas_call(
        functools.partial(exchange_kernel, chips, per_core, b2 is not None, final),
        out_shape=out_shape,
        in_specs=[vmem] * len(operands),
        out_specs=vmem if final else (vmem, vmem),
        scratch_shapes=scratch,
        compiler_params=pltpu.CompilerParams(collective_id=call_id, has_side_effects=True, vmem_limit_bytes=67043328),
        cost_estimate=pl.CostEstimate(flops=flops, bytes_accessed=40 << 20, transcendentals=0),
        name=f"exchange{call_id}",
    )(*operands)
    if final:
        return result.reshape(own, width)
    return result[0].reshape(seq_len, width2), result[1].reshape(own, width)


def attention_kernel(scale, block, q_ref, k_ref, v_ref, o_ref):
    seq_len = q_ref.shape[0]
    slope = scale * math.log2(math.e)
    row = lax.broadcasted_iota(jnp.int32, (block, block), 0)
    col = lax.broadcasted_iota(jnp.int32, (block, block), 1)
    contract = (((1,), (1,)), ((), ()))
    for start in range(0, seq_len, block):
        end = start + block
        q = q_ref[start:end]
        diag = lax.dot_general(q, k_ref[start:end], contract, preferred_element_type=F32)
        diag = jnp.where(row >= col, diag, -1e30)
        top = jnp.max(diag, axis=-1, keepdims=True)
        if start:
            past = lax.dot_general(q, k_ref[:start], contract, preferred_element_type=F32)
            top = jnp.maximum(top, jnp.max(past, axis=-1, keepdims=True))
        shift = top * slope
        diag = jnp.exp2(diag * slope - shift)
        total = jnp.sum(diag, axis=-1, keepdims=True)
        if start:
            past = jnp.exp2(past * slope - shift)
            total = total + jnp.sum(past, axis=-1, keepdims=True)
        inv = 1.0 / total
        out = jnp.dot((diag * inv).astype(BF16), v_ref[start:end], preferred_element_type=F32)
        if start:
            out = out + jnp.dot((past * inv).astype(BF16), v_ref[:start], preferred_element_type=F32)
        o_ref[start:end] = out.astype(BF16)


def attention(qkv, heads, scale):
    seq_len = qkv.shape[0]
    spec = lambda first: pl.BlockSpec((seq_len, LANES), lambda h: (0, first + h))
    return pl.pallas_call(
        functools.partial(attention_kernel, scale, 256),
        grid=(heads,),
        out_shape=jax.ShapeDtypeStruct((seq_len, heads * LANES), BF16),
        in_specs=[spec(0), spec(heads), spec(2 * heads)],
        out_specs=spec(0),
        compiler_params=pltpu.CompilerParams(vmem_limit_bytes=50 << 20),
        cost_estimate=pl.CostEstimate(flops=2 * heads * seq_len * seq_len * LANES, bytes_accessed=8 << 20, transcendentals=heads * seq_len * seq_len // 2),
        name="attention",
    )(qkv, qkv, qkv)


def solution(mesh):
    tp_size = mesh.shape["tp"]
    chips = tp_size // 2

    def local_forward(x_local, ln1_gain, ln1_bias, ln2_gain, ln2_bias, w_qkv, w_out, b_out, w_up, b_up, w_down, b_down):
        layers, width, _, heads, head_dim = w_qkv.shape
        scale = 1.0 / math.sqrt(head_dim)
        pad = LANES - head_dim
        wq = jnp.pad(w_qkv, ((0, 0), (0, 0), (0, 0), (0, 0), (0, pad))).reshape(layers, width, 3 * heads * LANES)
        wo = jnp.pad(w_out, ((0, 0), (0, 0), (0, pad), (0, 0))).reshape(layers, heads * LANES, width)
        resid = x_local[0].astype(F32)
        normed = layer_norm(resid, ln1_gain[0], ln1_bias[0])
        gathered = lax.all_gather(normed, "tp", axis=0, tiled=True)
        qkv = jnp.dot(gathered, wq[0], preferred_element_type=F32).astype(BF16)
        call_id = 0
        for layer in range(layers):
            heads_out = attention(qkv, heads, scale)
            hidden, resid = exchange(chips, call_id, heads_out, wo[layer], resid, b_out[layer],
                                     (ln2_gain[layer], ln2_bias[layer]), w_up[layer], b_up[layer])
            if layer + 1 < layers:
                qkv, resid = exchange(chips, call_id + 1, hidden, w_down[layer], resid, b_down[layer],
                                      (ln1_gain[layer + 1], ln1_bias[layer + 1]), wq[layer + 1])
            else:
                out = exchange(chips, call_id + 1, hidden, w_down[layer], resid, b_down[layer])
            call_id += 2
        return out[None]

    rows_spec = P("dp", "tp", None)
    in_specs = (rows_spec, P(), P(), P(), P(), P(None, None, None, "tp", None), P(None, "tp", None, None), P(), P(None, None, "tp"), P(None, "tp"), P(None, "tp", None), P())
    return jax.shard_map(local_forward, mesh=mesh, in_specs=in_specs, out_specs=rows_spec, check_vma=False)
```

time: 1630 us -> 909 us (0.56)
  waiting for transfers between devices: 839 us -> 55.5 us
  Pallas kernels: 0 us -> 753 us
  blocking collectives: 467 us -> 0 us
  matrix products: 234 us -> 22.3 us
  other arithmetic: 49.2 us -> 8.34 us
  local copies, waits for them, and re-layouts: 13.8 us -> 51.6 us
    pallas_call x0 -> x6, Pallas kernels: none -> 753 us  [the longest x4 703 us: exchange(): pl.pallas_call(functools.partial(exchange_kernel, chips, per_core, b2 is...]
    all_to_all x2 -> x0, blocking collectives: 467 us -> none  [scatter_rows(): received = lax.all_to_all(pieces, 'tp', 1, 1, tiled=True)]
    all_to_all x2 -> x0, waiting for transfers between devices: 455 us -> none  [scatter_rows(): received = lax.all_to_all(pieces, 'tp', 1, 1, tiled=True)]
    all_gather x4 -> x1, waiting for transfers between devices: 384 us -> 55.4 us  [local_forward(): gathered = lax.all_gather(normed, 'tp', axis=0, tiled=True)]
    dot_general x6 -> x1, matrix products: 132 us -> 22.3 us  [local_forward(): qkv = jnp.dot(gathered, wq[0], preferred_element_type=F32).astype(BF16)]
    sub x2 -> x0, matrix products: 72.8 us -> none  [local_forward(): jax.nn.softmax(jnp.where(causal, scores, -1e+30), axis=-1)]
    unnamed x2 -> x0, matrix products: 29.5 us -> none
    squeeze x0 -> x3, local copies, waits for them, and re-layouts: none -> 27.4 us  [the longest x1 11.6 us: local_forward(): w_up[layer]]
  transfers between devices with their start and end apart: 6 -> 1, of which waited for: 6 -> 1; matrix products, arithmetic and copies ran while one was open for 1% -> 5% of each run, Pallas kernels for 0% -> 0%
where the time goes in v1:
time: 909 us; the launch traced here: 904 us
  Pallas kernels  753 us (83%)
  waiting for transfers between devices  55.5 us (6%)
  local copies, waits for them, and re-layouts  51.6 us (6%)
  matrix products  22.3 us (2%)
  between operations  13.5 us (1%)
    pallas_call x4, Pallas kernels, exchange(): pl.pallas_call(functools.partial(exchange_kernel, chips, per_core, b2 is...  703 us
    all_gather x1, waiting for transfers between devices, local_forward(): gathered = lax.all_gather(normed, 'tp', axis=0, tiled=True)  55.4 us
    pallas_call x2, Pallas kernels, attention(): pl.pallas_call(functools.partial(attention_kernel, scale, 256), grid=(hea...  49.7 us
    dot_general x1, matrix products, local_forward(): qkv = jnp.dot(gathered, wq[0], preferred_element_type=F32).astype(BF16)  22.3 us
  transfers between devices with their start and end apart: 1, of which 1 were waited for; matrix products, arithmetic and copies ran while one was open for 5% of the time, Pallas kernels for 0%

profile of v1, /device:TPU:0, one launch (start us, length us, event | category | flops | bytes accessed | tf_op | source)
XLA Modules:
  0.0 904.1 jit_solution(13158591130882878696)
XLA Ops:
  6.5 1.7 convert_reduce_fusion
  8.2 1.8 multiply_reduce_fusion
  10.0 1.5 fusion.4
  11.5 2.9 add_convert_fusion
  14.5 1.9 convert.1.refs_2_
  16.4 10.3 %pad_slice_fusion = (bf16[1,2560,3,4,128]{1,4,3,2,0:T(8,128)(2,1)}, bf16[1,2560,3,4,128]{1,4,3,2,0:T(8,128)(2,1)}) fusion(bf16[2,2560,3,4,80]{1,4,3,2,0:T(8,128)(2,1)} %param.17), kind=kLoop, calls=%fused_computation | loop fusion | bytes 25559040 | tf_op jit(solution)/shard_map/slice | solution.py:318
  26.7 10.8 %copy.14.refs_6_ = bf16[2560,1536]{1,0:T(8,128)(2,1)} copy(bf16[2560,1536]{0,1:T(8,128)(2,1)} %bitcast.31) | data formatting | bytes 15728640 | tf_op jit(solution)/shard_map/squeeze | solution.py:318
  38.1 2.7 pad_slice_fusion.2
  41.5 0.6 fusion
  42.1 0.6 fusion.1
  42.8 11.6 %slice_bitcast_fusion.1 = (bf16[2560,1280]{1,0:T(8,128)(2,1)}, bf16[2560,1280]{1,0:T(8,128)(2,1)}) fusion(bf16[2,2560,1280]{2,1,0:T(8,128)(2,1)} %param.20), kind=kLoop, calls=%fused_computation.4 | loop fusion | bytes 26214400 | tf_op jit(solution)/shard_map/squeeze | solution.py:315
  54.4 1.5 slice-done.3
  55.8 5.0 slice_bitcast_fusion
  60.8 55.4 %all-gather.2.cloned.1.call-done = bf16[2048,2560]{1,0:T(8,128)(2,1)} async-done(((bf16[256,2560]{1,0:T(8,128)(2,1)}), bf16[2048,2560]{1,0:T(8,128)(2,1)}) %all-gather.2.cloned.1.call-update) | async-done | bytes 10485776 | tf_op jit(solution)/shard_map/all_gather | solution.py:309
  116.2 22.3 %convolution_convert_fusion.q_ref.k_ref.v_ref = bf16[2048,1536]{1,0:T(8,128)(2,1)} fusion(bf16[2048,2560]{1,0:T(8,128)(2,1)} %all-gather.2.cloned.1.call-done, bf16[2560,1536]{0,1:T(8,128)(2,1)} %bitcast.35), kind=kOutput, calls=%fused_computation.2 | convolution fusion | flops 16109273088 | bytes 24641536 | tf_op jit(solution)/shard_map/dot_general | solution.py:310
  138.5 24.9 %attention.2 = bf16[2048,512]{1,0:T(8,128)(2,1)S(1)} custom-call(bf16[2048,1536]{1,0:T(8,128)(2,1)} %convolution_convert_fusion.q_ref.k_ref.v_ref, bf16[2048,1536]{1,0:T(8,128)(2,1)} %convolution_convert_fusion.q_ref.k_ref.v_ref, bf16[2048,1536]{1,0:T(8,128)(2,1)} %convolution_convert_fusion.q_ref.k_ref.v_ref), custom_call_target="tpu_custom_call" | custom-call | flops 4294967296 | bytes 8388608 | tf_op jit(solution)/shard_map/attention/pallas_call | solution.py:285
  163.4 1.3 copy-done.1
  164.7 191.8 %exchange0.1 = (bf16[4,2,8,32,1280]{4,3,2,1,0:T(8,128)(2,1)}, f32[8,32,2560]{2,1,0:T(8,128)}) custom-call(bf16[4,2,8,32,512]{4,3,2,1,0:T(8,128)(2,1)} %bitcast.27, bf16[512,2560]{1,0:T(8,128)(2,1)} %bitcast.37, f32[8,32,2560]{2,1,0:T(8,128)} %convert.1.refs_2_, f32[1,2560]{1,0:T(1,128)} %get-tuple-element.32.refs_3_, f32[1,2560]{1,0:T(1,128)} %get-tuple-element.41.refs_4_, ...), custom_call_target="tpu_custom_call" | custom-call | flops 18790481920 | bytes 41943040 | tf_op jit(solution)/shard_map/exchange0/pallas_call | solution.py:239
  357.1 192.0 %exchange1.1 = (bf16[4,2,8,32,1536]{4,3,2,1,0:T(8,128)(2,1)}, f32[8,32,2560]{2,1,0:T(8,128)}) custom-call(bf16[4,2,8,32,1280]{4,3,2,1,0:T(8,128)(2,1)} %get-tuple-element.11.refs_0_, bf16[1280,2560]{1,0:T(8,128)(2,1)} %get-tuple-element.18.refs_1_, f32[8,32,2560]{2,1,0:T(8,128)} %get-tuple-element.12.refs_2_, f32[1,2560]{1,0:T(1,128)} %get-tuple-element.26.refs_3_, ...), custom_call_target="tpu_custom_call" | custom-call | flops 29527900160 | bytes 41943040 | tf_op jit(solution)/shard_map/exchange1/pallas_call | solution.py:239
  549.1 24.9 %attention.3 = bf16[2048,512]{1,0:T(8,128)(2,1)S(1)} custom-call(bf16[2048,1536]{1,0:T(8,128)(2,1)} %bitcast.28, bf16[2048,1536]{1,0:T(8,128)(2,1)} %bitcast.29, bf16[2048,1536]{1,0:T(8,128)(2,1)} %bitcast.30), custom_call_target="tpu_custom_call" | custom-call | flops 4294967296 | bytes 8388608 | tf_op jit(solution)/shard_map/attention/pallas_call | solution.py:285
  574.0 1.3 copy-done
  575.3 187.3 %exchange2.1 = (bf16[4,2,8,32,1280]{4,3,2,1,0:T(8,128)(2,1)}, f32[8,32,2560]{2,1,0:T(8,128)}) custom-call(bf16[4,2,8,32,512]{4,3,2,1,0:T(8,128)(2,1)} %bitcast.26, bf16[512,2560]{1,0:T(8,128)(2,1)} %bitcast.36, f32[8,32,2560]{2,1,0:T(8,128)} %get-tuple-element.14.refs_2_, f32[1,2560]{1,0:T(1,128)} %get-tuple-element.31.refs_3_, ...), custom_call_target="tpu_custom_call" | custom-call | flops 18790481920 | bytes 41943040 | tf_op jit(solution)/shard_map/exchange2/pallas_call | solution.py:239
  762.6 132.2 %exchange3.1 = bf16[8,32,2560]{2,1,0:T(8,128)(2,1)} custom-call(bf16[4,2,8,32,1280]{4,3,2,1,0:T(8,128)(2,1)} %get-tuple-element.15.refs_0_, bf16[1280,2560]{1,0:T(8,128)(2,1)} %get-tuple-element.17.refs_1_, f32[8,32,2560]{2,1,0:T(8,128)} %get-tuple-element.16.refs_2_, f32[1,2560]{1,0:T(1,128)} %get-tuple-element.25.refs_3_), custom_call_target="tpu_custom_call" | custom-call | flops 13421772800 | bytes 41943040 | tf_op jit(solution)/shard_map/exchange3/pallas_call | solution.py:239
  894.8 2.5 copy.16
  (31 shorter events, 1.9 us)
Async XLA Ops:
  6.5 7.9 copy-start.2
  6.5 109.7 %all-gather.2.cloned.1.call-start = ((), (), s32[]{:S(2)}) async-start(), calls=%async_computation | async-start | bytes 11796480 | tf_op jit(solution)/shard_map/all_gather | solution.py:309
  26.7 10.8 %copy-start.8 = (f32[2,1280]{1,0:T(2,128)S(1)}, f32[2,1280]{1,0:T(2,128)}, u32[]{:S(2)}) copy-start(f32[2,1280]{1,0:T(2,128)} %param.21) | copy-start | bytes 30724
  26.7 11.5 %copy-start.3 = (bf16[2,4,80,2560]{3,2,1,0:T(8,128)(2,1)S(1)}, bf16[2,4,80,2560]{3,2,1,0:T(8,128)(2,1)}, u32[]{:S(2)}) copy-start(bf16[2,4,80,2560]{3,2,1,0:T(8,128)(2,1)} %param.18) | copy-start | bytes 9830404
  37.5 3.4 copy-start.6
  37.5 4.0 copy-start.7
  37.5 4.6 copy-start.4
  37.5 4.6 copy-start.5
  38.1 16.2 %slice-start = ((s8[13107200]{0:T(1024)(128)(4,1)}), s8[524288]{0:T(1024)(128)(4,1)S(1)}, s32[]{:S(2)}) async-start(s8[13107200]{0:T(1024)(128)(4,1)} %bitcast.33), calls=%async_computation.1 | async-start | bytes 1048576
  42.8 11.6 %slice-start.1 = ((s8[13107200]{0:T(1024)(128)(4,1)}), s8[4194304]{0:T(1024)(128)(4,1)S(1)}, s32[]{:S(2)}) async-start(s8[13107200]{0:T(1024)(128)(4,1)} %bitcast.33), calls=%async_computation.2 | async-start | bytes 8388608
  42.8 11.6 %slice-start.2 = ((s8[13107200]{0:T(1024)(128)(4,1)}), s8[4194304]{0:T(1024)(128)(4,1)S(1)}, s32[]{:S(2)}) async-start(s8[13107200]{0:T(1024)(128)(4,1)} %bitcast.33), calls=%async_computation.3 | async-start | bytes 8388608
  42.8 13.1 %slice-start.3 = ((s8[13107200]{0:T(1024)(128)(4,1)}), s8[4194304]{0:T(1024)(128)(4,1)S(1)}, s32[]{:S(2)}) async-start(s8[13107200]{0:T(1024)(128)(4,1)} %bitcast.33), calls=%async_computation.4 | async-start | bytes 8388608
  163.4 1.3 copy-start.1
  574.0 1.3 copy-start
Sparse Core Ops, SparseCore 0:
  14.6 101.6 all-gather.1

commit v2 on v1

--- a/solution.py
+++ b/solution.py
@@ -10,8 +10,9 @@
 F32 = jnp.float32
 BF16 = jnp.bfloat16
 LANES = 128
-CHUNK = 32
-AHEAD = 2
+CHUNK = 16
+AHEAD = 4
+HOP = 4
 MESH = pl.DeviceIdType.MESH
 
 
@@ -26,10 +27,14 @@
     return [(start, min(tile, width - start)) for start in range(0, width, tile)]
 
 
-def chunk_place(j, chips, per_core):
-    turn = (j // 2) % chips
-    owner = jnp.where(turn % 2 == 0, turn // 2, chips - 1 - turn // 2)
-    return owner, (j // (2 * chips)) * 2 + j % 2
+def owner_of(turn, chips):
+    if isinstance(turn, int):
+        return turn // 2 if turn % 2 == 0 else chips - 1 - turn // 2
+    return jnp.where(turn % 2 == 0, turn // 2, chips - 1 - turn // 2)
+
+
+def chunk_place(j, chips):
+    return owner_of(j % chips, chips), j // chips
 
 
 def exchange_kernel(chips, per_core, act, final, *refs):
@@ -41,6 +46,7 @@
          acc_ref, normed, part_s, part_r, sum_s, inc_r, inc2_r, norm_r, left_s, right_s, mate_s, mate_r) = refs
     n_chunks = chips * per_core
     far = chips - 1
+    group_rows = chips * 2 * CHUNK
     group = lax.axis_index("dp")
     me = lax.axis_index("tp")
     z, core = me // 2, me % 2
@@ -66,13 +72,14 @@
     pl.semaphore_wait(barrier, 1 + has_left.astype(jnp.int32) + has_right.astype(jnp.int32))
 
     def matmul_in(j):
-        owner, place = chunk_place(j, chips, per_core)
-        rows = x_ref[owner, :, pl.ds(place, 2)].reshape(4 * CHUNK, x_ref.shape[-1])
+        place = j // chips
+        rows = x_ref[:, :, place].reshape(group_rows, x_ref.shape[-1])
         for start, width in col_tiles(w_ref.shape[1]):
             tile = jnp.dot(rows, w_ref[:, start : start + width], preferred_element_type=F32)
-            part[owner, :, pl.ds(place, 2), :, start : start + width] = tile.astype(BF16).reshape(2, 2, CHUNK, width)
-        for half in range(2):
-            remote(part.at[owner, 1 - core, place + half], other.at[owner, place + half], part_s.at[j + half], part_r.at[j + half], mate).start()
+            part[:, :, place, :, start : start + width] = tile.astype(BF16).reshape(chips, 2, CHUNK, width)
+        for turn in range(chips):
+            owner = owner_of(turn, chips)
+            remote(part.at[owner, 1 - core, place], other.at[owner, place], part_s.at[j + turn], part_r.at[j + turn], mate).start()
 
     def own_sum(j, owner, place):
         mine = part.at[owner, core, place]
@@ -142,48 +149,48 @@
         remote(rows, rows, mate_s.at[j], mate_r.at[j], mate).start()
 
     def matmul_out(j):
-        owner, place = chunk_place(j, chips, per_core)
-        for half in range(2):
-            rows = normed.at[owner, 1 - core, place + half]
-            remote(rows, rows, mate_s.at[j + half], mate_r.at[j + half], mate).wait_recv()
-        rows = normed[owner, :, pl.ds(place, 2)].reshape(4 * CHUNK, normed.shape[-1])
+        place = j // chips
+        for turn in range(chips):
+            rows = normed.at[owner_of(turn, chips), 1 - core, place]
+            remote(rows, rows, mate_s.at[j + turn], mate_r.at[j + turn], mate).wait_recv()
+        rows = normed[:, :, place].reshape(group_rows, normed.shape[-1])
         for start, width in col_tiles(w2_ref.shape[1]):
             tile = jnp.dot(rows, w2_ref[:, start : start + width], preferred_element_type=F32)
             if act:
                 tile = jax.nn.gelu(tile + b2_ref[:, start : start + width], approximate=True)
-            out_ref[owner, :, pl.ds(place, 2), :, start : start + width] = tile.astype(BF16).reshape(2, 2, CHUNK, width)
+            out_ref[:, :, place, :, start : start + width] = tile.astype(BF16).reshape(chips, 2, CHUNK, width)
 
     def at_distance(j, distance, step):
         inside = (j >= 0) & (j < n_chunks)
         safe = jnp.clip(j, 0, n_chunks - 1)
-        owner, place = chunk_place(safe, chips, per_core)
+        owner, place = chunk_place(safe, chips)
         pl.when(inside & (jnp.abs(z - owner) == distance))(lambda: step(safe, owner, place))
 
     def tick(t, carry):
         for distance in range(far, -1, -1):
-            at_distance(t - AHEAD - far + distance, distance, finish_sum if distance == 0 else pass_sum)
+            at_distance(t - AHEAD - HOP * (far - distance), distance, finish_sum if distance == 0 else pass_sum)
         if not final:
             for distance in range(1, chips):
-                at_distance(t - AHEAD - far - distance, distance, pass_norm)
-
-        @pl.when((t % 2 == 0) & (t < n_chunks))
-        def _():
-            matmul_in(jnp.clip(t, 0, n_chunks - 2))
+                at_distance(t - AHEAD - HOP * (far + distance), distance, pass_norm)
+
+        @pl.when((t % chips == 0) & (t < n_chunks))
+        def _():
+            matmul_in(jnp.clip(t, 0, n_chunks - chips))
 
         if not final:
-            late = t - AHEAD - 2 * far - 2
-
-            @pl.when((t % 2 == 0) & (late >= 0))
+            late = t - AHEAD - 2 * HOP * far - chips
+
+            @pl.when((late % chips == 0) & (late >= 0))
             def _():
-                matmul_out(jnp.clip(late, 0, n_chunks - 2))
+                matmul_out(jnp.clip(late, 0, n_chunks - chips))
 
         return carry
 
-    ticks = n_chunks + AHEAD + far if final else n_chunks + AHEAD + 2 * far + 1
+    ticks = n_chunks + AHEAD + HOP * far if final else n_chunks + AHEAD + 2 * HOP * far + 1
     lax.fori_loop(0, ticks, tick, 0)
 
     def drain(j, carry):
-        owner, place = chunk_place(j, chips, per_core)
+        owner, place = chunk_place(j, chips)
         mine = part.at[owner, core, place]
         remote(mine, other.at[owner, place], part_s.at[j], part_r.at[j], mate).wait_send()
 

time: 909 us -> 743 us (0.82)
  Pallas kernels: 753 us -> 591 us
    pallas_call x4, Pallas kernels: 703 us -> 542 us  [exchange(): pl.pallas_call(functools.partial(exchange_kernel, chips, per_core, b2 is...]
  transfers between devices with their start and end apart: 1 -> 1, of which waited for: 1 -> 1; matrix products, arithmetic and copies ran while one was open for 5% -> 6% of each run, Pallas kernels for 0% -> 0%
where the time goes in v2:
time: 743 us
  Pallas kernels  591 us (80%)
  waiting for transfers between devices  55.5 us (7%)
  local copies, waits for them, and re-layouts  51.6 us (7%)
  matrix products  22.3 us (3%)
  between operations  13.5 us (2%)
  other arithmetic  8.34 us (1%)
    pallas_call x4, Pallas kernels, exchange(): pl.pallas_call(functools.partial(exchange_kernel, chips, per_core, b2 is...  542 us
    all_gather x1, waiting for transfers between devices, local_forward(): gathered = lax.all_gather(normed, 'tp', axis=0, tiled=True)  55.4 us
    pallas_call x2, Pallas kernels, attention(): pl.pallas_call(functools.partial(attention_kernel, scale, 256), grid=(hea...  49.8 us
    dot_general x1, matrix products, local_forward(): qkv = jnp.dot(gathered, wq[0], preferred_element_type=F32).astype(BF16)  22.3 us
  transfers between devices with their start and end apart: 1, of which 1 were waited for; matrix products, arithmetic and copies ran while one was open for 6% of the time, Pallas kernels for 0%

profile of v2, /device:TPU:0, one launch (start us, length us, event | category | flops | bytes accessed | tf_op | source)
XLA Modules:
  0.0 742.6 jit_solution(12306298227556532246)
XLA Ops:
  6.5 1.7 convert_reduce_fusion
  8.2 1.8 multiply_reduce_fusion
  10.0 1.5 fusion.4
  11.5 2.9 add_convert_fusion
  14.5 1.9 convert.1.refs_2_
  16.4 10.3 %pad_slice_fusion = (bf16[1,2560,3,4,128]{1,4,3,2,0:T(8,128)(2,1)}, bf16[1,2560,3,4,128]{1,4,3,2,0:T(8,128)(2,1)}) fusion(bf16[2,2560,3,4,80]{1,4,3,2,0:T(8,128)(2,1)} %param.17), kind=kLoop, calls=%fused_computation | loop fusion | bytes 25559040 | tf_op jit(solution)/shard_map/slice | solution.py:325
  26.7 10.8 %copy.14.refs_6_ = bf16[2560,1536]{1,0:T(8,128)(2,1)} copy(bf16[2560,1536]{0,1:T(8,128)(2,1)} %bitcast.31) | data formatting | bytes 15728640 | tf_op jit(solution)/shard_map/squeeze | solution.py:325
  38.1 2.7 pad_slice_fusion.2
  41.5 0.6 fusion
  42.1 0.6 fusion.1
  42.8 11.6 %slice_bitcast_fusion.1 = (bf16[2560,1280]{1,0:T(8,128)(2,1)}, bf16[2560,1280]{1,0:T(8,128)(2,1)}) fusion(bf16[2,2560,1280]{2,1,0:T(8,128)(2,1)} %param.20), kind=kLoop, calls=%fused_computation.4 | loop fusion | bytes 26214400 | tf_op jit(solution)/shard_map/squeeze | solution.py:322
  54.4 1.5 slice-done.3
  55.8 5.0 slice_bitcast_fusion
  60.8 55.4 %all-gather.2.cloned.1.call-done = bf16[2048,2560]{1,0:T(8,128)(2,1)} async-done(((bf16[256,2560]{1,0:T(8,128)(2,1)}), bf16[2048,2560]{1,0:T(8,128)(2,1)}) %all-gather.2.cloned.1.call-update) | async-done | bytes 10485776 | tf_op jit(solution)/shard_map/all_gather | solution.py:316
  116.2 22.3 %convolution_convert_fusion.q_ref.k_ref.v_ref = bf16[2048,1536]{1,0:T(8,128)(2,1)} fusion(bf16[2048,2560]{1,0:T(8,128)(2,1)} %all-gather.2.cloned.1.call-done, bf16[2560,1536]{0,1:T(8,128)(2,1)} %bitcast.35), kind=kOutput, calls=%fused_computation.2 | convolution fusion | flops 16109273088 | bytes 24641536 | tf_op jit(solution)/shard_map/dot_general | solution.py:317
  138.5 24.9 %attention.2 = bf16[2048,512]{1,0:T(8,128)(2,1)S(1)} custom-call(bf16[2048,1536]{1,0:T(8,128)(2,1)} %convolution_convert_fusion.q_ref.k_ref.v_ref, bf16[2048,1536]{1,0:T(8,128)(2,1)} %convolution_convert_fusion.q_ref.k_ref.v_ref, bf16[2048,1536]{1,0:T(8,128)(2,1)} %convolution_convert_fusion.q_ref.k_ref.v_ref), custom_call_target="tpu_custom_call" | custom-call | flops 4294967296 | bytes 8388608 | tf_op jit(solution)/shard_map/attention/pallas_call | solution.py:292
  163.4 1.3 copy-done.1
  164.7 146.1 %exchange0.1 = (bf16[4,2,16,16,1280]{4,3,2,1,0:T(8,128)(2,1)}, f32[16,16,2560]{2,1,0:T(8,128)}) custom-call(bf16[4,2,16,16,512]{4,3,2,1,0:T(8,128)(2,1)} %bitcast.27, bf16[512,2560]{1,0:T(8,128)(2,1)} %bitcast.37, f32[16,16,2560]{2,1,0:T(8,128)} %convert.1.refs_2_, f32[1,2560]{1,0:T(1,128)} %get-tuple-element.32.refs_3_, ...), custom_call_target="tpu_custom_call" | custom-call | flops 18790481920 | bytes 41943040 | tf_op jit(solution)/shard_map/exchange0/pallas_call | solution.py:246
  311.5 149.5 %exchange1.1 = (bf16[4,2,16,16,1536]{4,3,2,1,0:T(8,128)(2,1)}, f32[16,16,2560]{2,1,0:T(8,128)}) custom-call(bf16[4,2,16,16,1280]{4,3,2,1,0:T(8,128)(2,1)} %get-tuple-element.11.refs_0_, bf16[1280,2560]{1,0:T(8,128)(2,1)} %get-tuple-element.18.refs_1_, f32[16,16,2560]{2,1,0:T(8,128)} %get-tuple-element.12.refs_2_, f32[1,2560]{1,0:T(1,128)} %get-tuple-element.26.refs_3_, ...), custom_call_target="tpu_custom_call" | custom-call | flops 29527900160 | bytes 41943040 | tf_op jit(solution)/shard_map/exchange1/pallas_call | solution.py:246
  461.0 24.9 %attention.3 = bf16[2048,512]{1,0:T(8,128)(2,1)S(1)} custom-call(bf16[2048,1536]{1,0:T(8,128)(2,1)} %bitcast.28, bf16[2048,1536]{1,0:T(8,128)(2,1)} %bitcast.29, bf16[2048,1536]{1,0:T(8,128)(2,1)} %bitcast.30), custom_call_target="tpu_custom_call" | custom-call | flops 4294967296 | bytes 8388608 | tf_op jit(solution)/shard_map/attention/pallas_call | solution.py:292
  485.9 1.3 copy-done
  487.2 146.0 %exchange2.1 = (bf16[4,2,16,16,1280]{4,3,2,1,0:T(8,128)(2,1)}, f32[16,16,2560]{2,1,0:T(8,128)}) custom-call(bf16[4,2,16,16,512]{4,3,2,1,0:T(8,128)(2,1)} %bitcast.26, bf16[512,2560]{1,0:T(8,128)(2,1)} %bitcast.36, f32[16,16,2560]{2,1,0:T(8,128)} %get-tuple-element.14.refs_2_, f32[1,2560]{1,0:T(1,128)} %get-tuple-element.31.refs_3_, ...), custom_call_target="tpu_custom_call" | custom-call | flops 18790481920 | bytes 41943040 | tf_op jit(solution)/shard_map/exchange2/pallas_call | solution.py:246
  633.2 100.1 %exchange3.1 = bf16[16,16,2560]{2,1,0:T(8,128)(2,1)} custom-call(bf16[4,2,16,16,1280]{4,3,2,1,0:T(8,128)(2,1)} %get-tuple-element.15.refs_0_, bf16[1280,2560]{1,0:T(8,128)(2,1)} %get-tuple-element.17.refs_1_, f32[16,16,2560]{2,1,0:T(8,128)} %get-tuple-element.16.refs_2_, f32[1,2560]{1,0:T(1,128)} %get-tuple-element.25.refs_3_), custom_call_target="tpu_custom_call" | custom-call | flops 13421772800 | bytes 41943040 | tf_op jit(solution)/shard_map/exchange3/pallas_call | solution.py:246
  733.3 2.5 copy.16
  (31 shorter events, 1.9 us)
Async XLA Ops:
  6.5 7.9 %copy-start.2 = (bf16[1,256,2560]{2,1,0:T(8,128)(2,1)S(1)}, bf16[1,256,2560]{2,1,0:T(8,128)(2,1)}, u32[]{:S(2)}) copy-start(bf16[1,256,2560]{2,1,0:T(8,128)(2,1)} %param.12) | copy-start | bytes 3932164
  6.5 109.7 %all-gather.2.cloned.1.call-start = ((), (), s32[]{:S(2)}) async-start(), calls=%async_computation | async-start | bytes 11796480 | tf_op jit(solution)/shard_map/all_gather | solution.py:316
  26.7 10.8 %copy-start.8 = (f32[2,1280]{1,0:T(2,128)S(1)}, f32[2,1280]{1,0:T(2,128)}, u32[]{:S(2)}) copy-start(f32[2,1280]{1,0:T(2,128)} %param.21) | copy-start | bytes 30724
  26.7 11.5 %copy-start.3 = (bf16[2,4,80,2560]{3,2,1,0:T(8,128)(2,1)S(1)}, bf16[2,4,80,2560]{3,2,1,0:T(8,128)(2,1)}, u32[]{:S(2)}) copy-start(bf16[2,4,80,2560]{3,2,1,0:T(8,128)(2,1)} %param.18) | copy-start | bytes 9830404
  37.5 3.4 copy-start.6
  37.5 4.0 copy-start.7
  37.5 4.6 copy-start.4
  37.5 4.6 copy-start.5
  38.1 16.2 %slice-start = ((s8[13107200]{0:T(1024)(128)(4,1)}), s8[524288]{0:T(1024)(128)(4,1)S(1)}, s32[]{:S(2)}) async-start(s8[13107200]{0:T(1024)(128)(4,1)} %bitcast.33), calls=%async_computation.1 | async-start | bytes 1048576
  42.8 11.6 %slice-start.1 = ((s8[13107200]{0:T(1024)(128)(4,1)}), s8[4194304]{0:T(1024)(128)(4,1)S(1)}, s32[]{:S(2)}) async-start(s8[13107200]{0:T(1024)(128)(4,1)} %bitcast.33), calls=%async_computation.2 | async-start | bytes 8388608
  42.8 11.6 %slice-start.2 = ((s8[13107200]{0:T(1024)(128)(4,1)}), s8[4194304]{0:T(1024)(128)(4,1)S(1)}, s32[]{:S(2)}) async-start(s8[13107200]{0:T(1024)(128)(4,1)} %bitcast.33), calls=%async_computation.3 | async-start | bytes 8388608
  42.8 13.1 %slice-start.3 = ((s8[13107200]{0:T(1024)(128)(4,1)}), s8[4194304]{0:T(1024)(128)(4,1)S(1)}, s32[]{:S(2)}) async-start(s8[13107200]{0:T(1024)(128)(4,1)} %bitcast.33), calls=%async_computation.4 | async-start | bytes 8388608
  163.4 1.3 copy-start.1
  485.9 1.3 copy-start
Sparse Core Ops, SparseCore 0:
  14.6 101.6 all-gather.1

commit v3 on v2

v3 whole, which is shorter than its diff:
```python
import functools
import math
import jax
import jax.numpy as jnp
from jax import lax
from jax.experimental import pallas as pl
from jax.experimental.pallas import tpu as pltpu
from jax.sharding import PartitionSpec as P

F32 = jnp.float32
BF16 = jnp.bfloat16
LANES = 128
CHUNK = 16
AHEAD = 4
HOP = 4
MESH = pl.DeviceIdType.MESH


def layer_norm(resid, gain, shift):
    row_mean = jnp.mean(resid, axis=-1, keepdims=True)
    centered = resid - row_mean
    variance = jnp.mean(centered * centered, axis=-1, keepdims=True)
    return (centered * lax.rsqrt(variance + 1e-5) * gain + shift).astype(BF16)


def col_tiles(width, tile=512):
    return [(start, min(tile, width - start)) for start in range(0, width, tile)]


def owner_of(turn, chips):
    if isinstance(turn, int):
        return turn // 2 if turn % 2 == 0 else chips - 1 - turn // 2
    return jnp.where(turn % 2 == 0, turn // 2, chips - 1 - turn // 2)


def chunk_place(j, chips):
    return owner_of(j % chips, chips), j // chips


class Stage:
    def __init__(self, start, bufs, sems, bias, gain=None, shift=None):
        self.start, self.bias, self.gain, self.shift = start, bias, gain, shift
        self.final = gain is None
        self.part, self.other, self.inc, self.inc2 = bufs[:4]
        self.part_s, self.part_r, self.sum_s, self.inc_r, self.inc2_r = sems[:5]
        if not self.final:
            self.normed = bufs[4]
            self.norm_r, self.left_s, self.right_s, self.mate_s, self.mate_r = sems[5:]


def layer_kernel(chips, per_core, span, layer, final, *refs):
    refs = list(refs)
    take = lambda n: [refs.pop(0) for _ in range(n)]
    x_hbm, resid_hbm, w_out_hbm, w_up_hbm, w_down_hbm, bias_a, gain_a, shift_a, b_up, bias_b = take(10)
    if final:
        (y_ref,) = take(1)
    else:
        w_qkv_hbm, gain_b, shift_b, qkv_hbm, resid = take(5)
    x_ref, w_out, w_up, w_down, hidden, acc_ref, copy_s = take(7)
    stage_a = Stage(0, take(5), take(10), bias_a, gain_a, shift_a)
    if final:
        stage_b = Stage(span, take(4), take(5), bias_b)
        (resid,) = take(1)
    else:
        stage_b = Stage(span, take(5), take(10), bias_b, gain_b, shift_b)
        w_qkv, qkv_buf, qkv_s = take(3)
    n_chunks = chips * per_core
    far = chips - 1
    ring = span // chips
    group_rows = chips * 2 * CHUNK
    group = lax.axis_index("dp")
    me = lax.axis_index("tp")
    z, core = me // 2, me % 2
    mate = (group, z * 2 + (1 - core))
    left = (group, jnp.maximum(me - 2, 0))
    right = (group, jnp.minimum(me + 2, 2 * chips - 1))
    has_left, has_right = z > 0, z < far

    loads = [(x_hbm, x_ref), (w_out_hbm, w_out), (resid_hbm, resid), (w_up_hbm.at[layer], w_up), (w_down_hbm.at[layer], w_down)]
    if not final:
        loads.append((w_qkv_hbm, w_qkv))
    loads = [pltpu.make_async_copy(src, dst, copy_s.at[i]) for i, (src, dst) in enumerate(loads)]
    for load in loads:
        load.start()

    def remote(src, dst, send, recv, device):
        return pltpu.make_async_remote_copy(src_ref=src, dst_ref=dst, send_sem=send, recv_sem=recv, device_id=device, device_id_type=MESH)

    barrier = pltpu.get_barrier_semaphore()
    pl.semaphore_signal(barrier, inc=1, device_id=mate, device_id_type=MESH)

    @pl.when(has_left)
    def _():
        pl.semaphore_signal(barrier, inc=1, device_id=left, device_id_type=MESH)

    @pl.when(has_right)
    def _():
        pl.semaphore_signal(barrier, inc=1, device_id=right, device_id_type=MESH)

    pl.semaphore_wait(barrier, 1 + has_left.astype(jnp.int32) + has_right.astype(jnp.int32))
    for load in loads[:3]:
        load.wait()

    def store_part(s, j, rows, w_ref):
        at = (j // chips) % ring
        for start, width in col_tiles(w_ref.shape[1]):
            tile = jnp.dot(rows, w_ref[:, start : start + width], preferred_element_type=F32)
            s.part[:, :, at, :, start : start + width] = tile.astype(BF16).reshape(chips, 2, CHUNK, width)
        for turn in range(chips):
            owner, n = owner_of(turn, chips), (j + turn) % span
            remote(s.part.at[owner, 1 - core, at], s.other.at[owner, at], s.part_s.at[n], s.part_r.at[n], mate).start()

    def own_sum(s, n, owner, at):
        mine = s.part.at[owner, core, at]
        remote(mine, s.other.at[owner, at], s.part_s.at[n], s.part_r.at[n], mate).wait_recv()
        acc_ref[...] = mine[...].astype(F32) + s.other[owner, at].astype(F32)

    def add_inc(s, n, owner, at):
        remote(s.inc.at[owner, at], s.inc.at[owner, at], s.sum_s.at[n], s.inc_r.at[n], left).wait_recv()
        acc_ref[...] += s.inc[owner, at].astype(F32)

    def pass_sum(s, n, owner, place):
        at = place % ring
        own_sum(s, n, owner, at)

        @pl.when(jnp.where(z < owner, has_left, has_right))
        def _():
            add_inc(s, n, owner, at)

        mine = s.part.at[owner, core, at]
        mine[...] = acc_ref[...].astype(BF16)

        @pl.when(z < owner)
        def _():
            remote(mine, s.inc.at[owner, at], s.sum_s.at[n], s.inc_r.at[n], right).start()

        @pl.when(z > owner + 1)
        def _():
            remote(mine, s.inc.at[owner, at], s.sum_s.at[n], s.inc_r.at[n], left).start()

        @pl.when(z == owner + 1)
        def _():
            remote(mine, s.inc2.at[at], s.sum_s.at[n], s.inc2_r.at[n], left).start()

    def send_left(s, n, rows):
        remote(rows, rows, s.left_s.at[n], s.norm_r.at[n], left).start()

    def send_right(s, n, rows):
        remote(rows, rows, s.right_s.at[n], s.norm_r.at[n], right).start()

    def finish_sum(s, n, owner, place):
        at = place % ring
        own_sum(s, n, owner, at)

        @pl.when(has_left)
        def _():
            add_inc(s, n, owner, at)

        @pl.when(has_right)
        def _():
            remote(s.inc2.at[at], s.inc2.at[at], s.sum_s.at[n], s.inc2_r.at[n], right).wait_recv()
            acc_ref[...] += s.inc2[at].astype(F32)

        total = resid[place] + (acc_ref[...] + s.bias[...])
        if s.final:
            y_ref[place] = total.astype(BF16)
            return
        resid[place] = total
        rows = s.normed.at[owner, core, at]
        rows[...] = layer_norm(total, s.gain[...], s.shift[...])
        pl.when(has_left)(lambda: send_left(s, n, rows))
        pl.when(has_right)(lambda: send_right(s, n, rows))
        remote(rows, rows, s.mate_s.at[n], s.mate_r.at[n], mate).start()

    def pass_norm(s, n, owner, place):
        rows = s.normed.at[owner, core, place % ring]
        remote(rows, rows, s.left_s.at[n], s.norm_r.at[n], left).wait_recv()
        pl.when((z < owner) & has_left)(lambda: send_left(s, n, rows))
        pl.when((z > owner) & has_right)(lambda: send_right(s, n, rows))
        remote(rows, rows, s.mate_s.at[n], s.mate_r.at[n], mate).start()

    def normed_rows(s, j):
        at = (j // chips) % ring
        for turn in range(chips):
            rows, n = s.normed.at[owner_of(turn, chips), 1 - core, at], (j + turn) % span
            remote(rows, rows, s.mate_s.at[n], s.mate_r.at[n], mate).wait_recv()
        return s.normed[:, :, at].reshape(group_rows, s.normed.shape[-1])

    def release(s, j):
        at = (j // chips) % ring
        for turn in range(chips):
            owner, n = owner_of(turn, chips), (j + turn) % span
            mine = s.part.at[owner, core, at]
            remote(mine, s.other.at[owner, at], s.part_s.at[n], s.part_r.at[n], mate).wait_send()
            pl.when(z != owner)(remote(mine, s.inc.at[owner, at], s.sum_s.at[n], s.inc_r.at[n], left).wait_send)
            if not s.final:
                rows = s.normed.at[owner, core, at]
                pl.when((z <= owner) & has_left)(remote(rows, rows, s.left_s.at[n], s.norm_r.at[n], left).wait_send)
                pl.when((z >= owner) & has_right)(remote(rows, rows, s.right_s.at[n], s.norm_r.at[n], right).wait_send)
                remote(rows, rows, s.mate_s.at[n], s.mate_r.at[n], mate).wait_send()

    def project_out(j):
        pl.when(j >= span)(lambda: release(stage_a, j - span))
        store_part(stage_a, j, x_ref[:, :, j // chips].reshape(group_rows, x_ref.shape[-1]), w_out)

    def mlp(j):
        @pl.when(j == 0)
        def _():
            loads[3].wait()
            loads[4].wait()

        rows = normed_rows(stage_a, j)
        for start, width in col_tiles(w_up.shape[1]):
            tile = jnp.dot(rows, w_up[:, start : start + width], preferred_element_type=F32)
            hidden[:, start : start + width] = jax.nn.gelu(tile + b_up[:, start : start + width], approximate=True).astype(BF16)
        pl.when(j >= span)(lambda: release(stage_b, j - span))
        store_part(stage_b, j, hidden[...], w_down)

    def qkv_copy(place):
        return pltpu.make_async_copy(qkv_buf.at[place % 2], qkv_hbm.at[:, :, place], qkv_s.at[place % 2])

    def project_qkv(j):
        place = j // chips
        pl.when(j == 0)(lambda: loads[5].wait())
        pl.when(place >= 2)(lambda: qkv_copy(place - 2).wait())
        rows = normed_rows(stage_b, j)
        for start, width in col_tiles(w_qkv.shape[1]):
            tile = jnp.dot(rows, w_qkv[:, start : start + width], preferred_element_type=F32)
            qkv_buf[place % 2, :, :, :, start : start + width] = tile.astype(BF16).reshape(chips, 2, CHUNK, width)
        qkv_copy(place).start()

    def at_distance(s, j, distance, step):
        inside = (j >= 0) & (j < n_chunks)
        safe = jnp.clip(j, 0, n_chunks - 1)
        owner, place = chunk_place(safe, chips)
        pl.when(inside & (jnp.abs(z - owner) == distance))(lambda: step(s, safe % span, owner, place))

    def at_group(j, step):
        pl.when((j >= 0) & (j < n_chunks) & (j % chips == 0))(lambda: step(jnp.clip(j, 0, n_chunks - chips)))

    def tick(t, carry):
        for s in (stage_b, stage_a):
            for distance in range(far, -1, -1):
                at_distance(s, t - s.start - AHEAD - HOP * (far - distance), distance, finish_sum if distance == 0 else pass_sum)
            if not s.final:
                for distance in range(1, chips):
                    at_distance(s, t - s.start - AHEAD - HOP * (far + distance), distance, pass_norm)
        if not final:
            at_group(t - 2 * span, project_qkv)
        at_group(t - span, mlp)
        at_group(t, project_out)
        return carry

    ticks = span + n_chunks + AHEAD + HOP * far if final else 2 * span + n_chunks - chips + 1
    lax.fori_loop(0, ticks, tick, 0)

    def drain(i, carry):
        release(stage_a, n_chunks - span + i * chips)
        release(stage_b, n_chunks - span + i * chips)
        return carry

    lax.fori_loop(0, ring, drain, 0)
    if not final:
        qkv_copy(per_core - 2).wait()
        qkv_copy(per_core - 1).wait()


def layer_tail(chips, layer, x, resid, w_out, w_up, w_down, bias_a, norm_a, b_up, bias_b, norm_b=None, w_qkv=None):
    seq_len, depth = x.shape
    own, width = resid.shape
    mid = w_up.shape[2]
    per_core = own // CHUNK
    final = norm_b is None
    span = AHEAD + 2 * HOP * (chips - 1) + chips
    ring = span // chips
    assert span % chips == 0 and per_core >= ring
    blocks = (chips, 2, per_core, CHUNK)
    any_spec = pl.BlockSpec(memory_space=pl.ANY)
    vmem = pl.BlockSpec(memory_space=pltpu.VMEM)
    operands = [x.reshape(*blocks, depth), resid.reshape(per_core, CHUNK, width), w_out, w_up, w_down,
                bias_a[None], norm_a[0][None], norm_a[1][None], b_up[None], bias_b[None]]
    in_specs = [any_spec] * 5 + [vmem] * 5
    sems = [pltpu.SemaphoreType.DMA((span,))]
    slots = [
        pltpu.VMEM((chips, 2, ring, CHUNK, width), BF16),
        pltpu.VMEM((chips, ring, CHUNK, width), BF16),
        pltpu.VMEM((chips, ring, CHUNK, width), BF16),
        pltpu.VMEM((ring, CHUNK, width), BF16),
    ]
    norm_slots = [pltpu.VMEM((chips, 2, ring, CHUNK, width), BF16)]
    scratch = [
        pltpu.VMEM((*blocks, depth), BF16),
        pltpu.VMEM((depth, width), BF16),
        pltpu.VMEM((width, mid), BF16),
        pltpu.VMEM((mid, width), BF16),
        pltpu.VMEM((chips * 2 * CHUNK, mid), BF16),
        pltpu.VMEM((CHUNK, width), F32),
        pltpu.SemaphoreType.DMA((6,)),
    ] + slots + norm_slots + sems * 10
    flops = 2 * seq_len * width * (depth + 2 * mid)
    if final:
        out_shape = jax.ShapeDtypeStruct((per_core, CHUNK, width), BF16)
        out_specs = vmem
        scratch += slots + sems * 5 + [pltpu.VMEM((per_core, CHUNK, width), F32)]
    else:
        width2 = w_qkv.shape[1]
        operands += [w_qkv, norm_b[0][None], norm_b[1][None]]
        in_specs += [any_spec, vmem, vmem]
        out_shape = (jax.ShapeDtypeStruct((*blocks, width2), BF16), jax.ShapeDtypeStruct((per_core, CHUNK, width), F32))
        out_specs = (any_spec, vmem)
        scratch += slots + norm_slots + sems * 10
        scratch += [pltpu.VMEM((width, width2), BF16), pltpu.VMEM((2, chips, 2, CHUNK, width2), BF16), pltpu.SemaphoreType.DMA((2,))]
        flops += 2 * seq_len * width * width2
    result = pl.pallas_call(
        functools.partial(layer_kernel, chips, per_core, span, layer, final),
        out_shape=out_shape,
        in_specs=in_specs,
        out_specs=out_specs,
        scratch_shapes=scratch,
        compiler_params=pltpu.CompilerParams(collective_id=layer, has_side_effects=True, vmem_limit_bytes=67043328),
        cost_estimate=pl.CostEstimate(flops=flops, bytes_accessed=40 << 20, transcendentals=0),
        name=f"layer{layer}",
    )(*operands)
    if final:
        return result.reshape(own, width)
    return result[0].reshape(seq_len, width2), result[1].reshape(own, width)


def attention_kernel(scale, block, q_ref, k_ref, v_ref, o_ref):
    seq_len = q_ref.shape[0]
    slope = scale * math.log2(math.e)
    row = lax.broadcasted_iota(jnp.int32, (block, block), 0)
    col = lax.broadcasted_iota(jnp.int32, (block, block), 1)
    contract = (((1,), (1,)), ((), ()))
    for start in range(0, seq_len, block):
        end = start + block
        q = q_ref[start:end]
        diag = lax.dot_general(q, k_ref[start:end], contract, preferred_element_type=F32)
        diag = jnp.where(row >= col, diag, -1e30)
        top = jnp.max(diag, axis=-1, keepdims=True)
        if start:
            past = lax.dot_general(q, k_ref[:start], contract, preferred_element_type=F32)
            top = jnp.maximum(top, jnp.max(past, axis=-1, keepdims=True))
        shift = top * slope
        diag = jnp.exp2(diag * slope - shift)
        total = jnp.sum(diag, axis=-1, keepdims=True)
        if start:
            past = jnp.exp2(past * slope - shift)
            total = total + jnp.sum(past, axis=-1, keepdims=True)
        inv = 1.0 / total
        out = jnp.dot((diag * inv).astype(BF16), v_ref[start:end], preferred_element_type=F32)
        if start:
            out = out + jnp.dot((past * inv).astype(BF16), v_ref[:start], preferred_element_type=F32)
        o_ref[start:end] = out.astype(BF16)


def attention(qkv, heads, scale):
    seq_len = qkv.shape[0]
    spec = lambda first: pl.BlockSpec((seq_len, LANES), lambda h: (0, first + h))
    return pl.pallas_call(
        functools.partial(attention_kernel, scale, 256),
        grid=(heads,),
        out_shape=jax.ShapeDtypeStruct((seq_len, heads * LANES), BF16),
        in_specs=[spec(0), spec(heads), spec(2 * heads)],
        out_specs=spec(0),
        compiler_params=pltpu.CompilerParams(vmem_limit_bytes=50 << 20),
        cost_estimate=pl.CostEstimate(flops=2 * heads * seq_len * seq_len * LANES, bytes_accessed=8 << 20, transcendentals=heads * seq_len * seq_len // 2),
        name="attention",
    )(qkv, qkv, qkv)


def solution(mesh):
    tp_size = mesh.shape["tp"]
    chips = tp_size // 2

    def local_forward(x_local, ln1_gain, ln1_bias, ln2_gain, ln2_bias, w_qkv, w_out, b_out, w_up, b_up, w_down, b_down):
        layers, width, _, heads, head_dim = w_qkv.shape
        scale = 1.0 / math.sqrt(head_dim)
        pad = LANES - head_dim
        wq = jnp.pad(w_qkv, ((0, 0), (0, 0), (0, 0), (0, 0), (0, pad))).reshape(layers, width, 3 * heads * LANES)
        wo = jnp.pad(w_out, ((0, 0), (0, 0), (0, pad), (0, 0))).reshape(layers, heads * LANES, width)
        resid = x_local[0].astype(F32)
        normed = layer_norm(resid, ln1_gain[0], ln1_bias[0])
        gathered = lax.all_gather(normed, "tp", axis=0, tiled=True)
        qkv = jnp.dot(gathered, wq[0], preferred_element_type=F32).astype(BF16)
        for layer in range(layers):
            heads_out = attention(qkv, heads, scale)
            args = (chips, layer, heads_out, resid, wo[layer], w_up, w_down, b_out[layer],
                    (ln2_gain[layer], ln2_bias[layer]), b_up[layer], b_down[layer])
            if layer + 1 < layers:
                qkv, resid = layer_tail(*args, (ln1_gain[layer + 1], ln1_bias[layer + 1]), wq[layer + 1])
            else:
                out = layer_tail(*args)
        return out[None]

    rows_spec = P("dp", "tp", None)
    in_specs = (rows_spec, P(), P(), P(), P(), P(None, None, None, "tp", None), P(None, "tp", None, None), P(), P(None, None, "tp"), P(None, "tp"), P(None, "tp", None), P())
    return jax.shard_map(local_forward, mesh=mesh, in_specs=in_specs, out_specs=rows_spec, check_vma=False)
```

time: 743 us -> 676 us (0.910)
  Pallas kernels: 591 us -> 527 us
  local copies, waits for them, and re-layouts: 51.6 us -> 31.8 us
  waiting for transfers between devices: 55.5 us -> 73.8 us
    pallas_call x4 -> x2, Pallas kernels: 542 us -> 477 us  [layer_tail(): pl.pallas_call(functools.partial(layer_kernel, chips, per_core, span, lay...]
    all_gather x1, waiting for transfers between devices: 55.4 us -> 73.8 us  [local_forward(): gathered = lax.all_gather(normed, 'tp', axis=0, tiled=True)]
    squeeze x2 -> x0, local copies, waits for them, and re-layouts: 16.6 us -> none  [the longest x1 11.6 us: local_forward(): w_up[layer]]
  transfers between devices with their start and end apart: 1 -> 1, of which waited for: 1 -> 1; matrix products, arithmetic and copies ran while one was open for 6% -> 4% of each run, Pallas kernels for 0% -> 0%
where the time goes in v3:
time: 676 us; the launch traced here: 675 us
  Pallas kernels  527 us (78%)
  waiting for transfers between devices  73.8 us (11%)
  local copies, waits for them, and re-layouts  31.8 us (5%)
  matrix products  22.2 us (3%)
  between operations  13.5 us (2%)
  other arithmetic  6.97 us (1%)
    pallas_call x2, Pallas kernels, layer_tail(): pl.pallas_call(functools.partial(layer_kernel, chips, per_core, span, lay...  477 us
    all_gather x1, waiting for transfers between devices, local_forward(): gathered = lax.all_gather(normed, 'tp', axis=0, tiled=True)  73.8 us
    pallas_call x2, Pallas kernels, attention(): pl.pallas_call(functools.partial(attention_kernel, scale, 256), grid=(hea...  49.8 us
    dot_general x1, matrix products, local_forward(): qkv = jnp.dot(gathered, wq[0], preferred_element_type=F32).astype(BF16)  22.2 us
  transfers between devices with their start and end apart: 1, of which 1 were waited for; matrix products, arithmetic and copies ran while one was open for 4% of the time, Pallas kernels for 0%

profile of v3, /device:TPU:0, one launch (start us, length us, event | category | flops | bytes accessed | tf_op | source)
XLA Modules:
  0.0 675.3 jit_solution(8245999553416093030)
XLA Ops:
  6.5 0.0 all-gather.2.cloned.1.call-start
  6.5 1.7 convert_reduce_fusion
  8.2 1.8 multiply_reduce_fusion
  10.0 0.0 copy-done.9
  10.1 0.6 fusion.4
  10.7 1.6 add_convert_fusion
  12.3 0.0 all-gather.2.cloned.1.call-update
  12.3 10.4 %pad_slice_fusion = (bf16[1,2560,3,4,128]{1,4,3,2,0:T(8,128)(2,1)}, bf16[1,2560,3,4,128]{1,4,3,2,0:T(8,128)(2,1)}) fusion(bf16[2,2560,3,4,80]{1,4,3,2,0:T(8,128)(2,1)} %param.17), kind=kLoop, calls=%fused_computation | loop fusion | bytes 25559040 | tf_op jit(solution)/shard_map/slice | solution.py:391
  22.7 10.7 %copy.14.refs_10_ = bf16[2560,1536]{1,0:T(8,128)(2,1)} copy(bf16[2560,1536]{0,1:T(8,128)(2,1)} %bitcast.23) | data formatting | bytes 15728640 | tf_op jit(solution)/shard_map/squeeze | solution.py:391
  33.4 1.9 convert.1.refs_1_
  35.2 0.6 fusion.6
  35.8 0.4 copy-done.3
  36.3 2.7 pad_slice_fusion.2
  39.0 0.6 fusion
  39.7 0.6 fusion.2
  40.3 73.8 %all-gather.2.cloned.1.call-done = bf16[2048,2560]{1,0:T(8,128)(2,1)} async-done(((bf16[256,2560]{1,0:T(8,128)(2,1)}), bf16[2048,2560]{1,0:T(8,128)(2,1)}) %all-gather.2.cloned.1.call-update) | async-done | bytes 10485776 | tf_op jit(solution)/shard_map/all_gather | solution.py:384
  114.1 22.2 %convolution_convert_fusion.q_ref.k_ref.v_ref = bf16[2048,1536]{1,0:T(8,128)(2,1)} fusion(bf16[2048,2560]{1,0:T(8,128)(2,1)} %all-gather.2.cloned.1.call-done, bf16[2560,1536]{0,1:T(8,128)(2,1)} %bitcast.25), kind=kOutput, calls=%fused_computation.2 | convolution fusion | flops 16109273088 | bytes 24641536 | tf_op jit(solution)/shard_map/dot_general | solution.py:385
  136.3 24.9 %attention.2 = bf16[2048,512]{1,0:T(8,128)(2,1)S(1)} custom-call(bf16[2048,1536]{1,0:T(8,128)(2,1)} %convolution_convert_fusion.q_ref.k_ref.v_ref, bf16[2048,1536]{1,0:T(8,128)(2,1)} %convolution_convert_fusion.q_ref.k_ref.v_ref, bf16[2048,1536]{1,0:T(8,128)(2,1)} %convolution_convert_fusion.q_ref.k_ref.v_ref), custom_call_target="tpu_custom_call" | custom-call | flops 4294967296 | bytes 8388608 | tf_op jit(solution)/shard_map/attention/pallas_call | solution.py:360
  161.2 1.3 copy-done
  162.5 265.7 %layer0.1 = (bf16[4,2,16,16,1536]{4,3,2,1,0:T(8,128)(2,1)}, f32[16,16,2560]{2,1,0:T(8,128)}) custom-call(bf16[4,2,16,16,512]{4,3,2,1,0:T(8,128)(2,1)} %bitcast.18, f32[16,16,2560]{2,1,0:T(8,128)} %convert.1.refs_1_, bf16[512,2560]{1,0:T(8,128)(2,1)} %bitcast.27, bf16[2,2560,1280]{2,1,0:T(8,128)(2,1)} %refs_3_.3, bf16[2,1280,2560]{2,1,0:T(8,128)(2,1)} %refs_4_.3, ...), custom_call_target="tpu_custom_call" | custom-call | flops 48318382080 | bytes 41943040 | tf_op jit(solution)/shard_map/layer0/pallas_call | solution.py:314
  428.3 24.9 %attention.3 = bf16[2048,512]{1,0:T(8,128)(2,1)S(1)} custom-call(bf16[2048,1536]{1,0:T(8,128)(2,1)} %bitcast.20, bf16[2048,1536]{1,0:T(8,128)(2,1)} %bitcast.21, bf16[2048,1536]{1,0:T(8,128)(2,1)} %bitcast.22), custom_call_target="tpu_custom_call" | custom-call | flops 4294967296 | bytes 8388608 | tf_op jit(solution)/shard_map/attention/pallas_call | solution.py:360
  453.2 1.3 copy-done.1
  454.5 211.5 %layer1.1 = bf16[16,16,2560]{2,1,0:T(8,128)(2,1)} custom-call(bf16[4,2,16,16,512]{4,3,2,1,0:T(8,128)(2,1)} %bitcast.19, f32[16,16,2560]{2,1,0:T(8,128)} %get-tuple-element.8.refs_1_, bf16[512,2560]{1,0:T(8,128)(2,1)} %bitcast.26, bf16[2,2560,1280]{2,1,0:T(8,128)(2,1)} %refs_3_.3, bf16[2,1280,2560]{2,1,0:T(8,128)(2,1)} %refs_4_.3, ...), custom_call_target="tpu_custom_call" | custom-call | flops 32212254720 | bytes 41943040 | tf_op jit(solution)/shard_map/layer1/pallas_call | solution.py:314
  666.0 2.5 copy.16
  (20 shorter events, 0.0 us)
Async XLA Ops:
  6.5 4.2 copy-start.2
  6.5 3.5 copy-start.9
  6.5 3.5 copy-start.8
  6.5 107.6 %all-gather.2.cloned.1.call-start = ((), (), s32[]{:S(2)}) async-start(), calls=%async_computation | async-start | bytes 11796480 | tf_op jit(solution)/shard_map/all_gather | solution.py:384
  33.4 1.9 copy-start.10
  33.4 2.9 copy-start.3
  36.3 2.7 copy-start.4
  36.3 2.7 copy-start.5
  36.3 3.4 copy-start.6
  36.3 3.4 copy-start.7
  161.2 1.3 copy-start
  453.2 1.3 copy-start.1
Sparse Core Ops, SparseCore 0:
  12.5 101.6 all-gather.1

commit v4 on v3

--- a/solution.py
+++ b/solution.py
@@ -326,44 +326,59 @@
     return result[0].reshape(seq_len, width2), result[1].reshape(own, width)
 
 
-def attention_kernel(scale, block, q_ref, k_ref, v_ref, o_ref):
+def attention_kernel(scale, block, step, q_ref, k_ref, v_ref, o_ref):
     seq_len = q_ref.shape[0]
     slope = scale * math.log2(math.e)
-    row = lax.broadcasted_iota(jnp.int32, (block, block), 0)
-    col = lax.broadcasted_iota(jnp.int32, (block, block), 1)
-    contract = (((1,), (1,)), ((), ()))
+    last = (((1,), (1,)), ((), ()))
+    first = (((0,), (0,)), ((), ()))
+    key = lax.broadcasted_iota(jnp.int32, (step, block), 0)
+    query = lax.broadcasted_iota(jnp.int32, (step, block), 1)
+
+    def weigh(start, end, probs):
+        return lax.dot_general(v_ref[start:end], probs.astype(BF16), first, preferred_element_type=F32)
+
+    def update(whole, skip, new, combine):
+        if whole is None:
+            return new
+        if skip == 0:
+            return combine(whole, new)
+        return jnp.concatenate([whole[:, :skip], combine(whole[:, skip:], new)], axis=1)
+
     for start in range(0, seq_len, block):
-        end = start + block
-        q = q_ref[start:end]
-        diag = lax.dot_general(q, k_ref[start:end], contract, preferred_element_type=F32)
-        diag = jnp.where(row >= col, diag, -1e30)
-        top = jnp.max(diag, axis=-1, keepdims=True)
+        q = q_ref[start : start + block]
+        top = past = total = out = None
+        near = []
+        for skip in range(0, block, step):
+            keys = k_ref[start + skip : start + skip + step]
+            scores = lax.dot_general(keys, q[skip:], last, preferred_element_type=F32)
+            scores = jnp.where(key[:, : block - skip] <= query[:, : block - skip], scores, -1e30)
+            near.append(scores)
+            top = update(top, skip, jnp.max(scores, axis=0, keepdims=True), jnp.maximum)
         if start:
-            past = lax.dot_general(q, k_ref[:start], contract, preferred_element_type=F32)
-            top = jnp.maximum(top, jnp.max(past, axis=-1, keepdims=True))
+            past = lax.dot_general(k_ref[:start], q, last, preferred_element_type=F32)
+            top = jnp.maximum(top, jnp.max(past, axis=0, keepdims=True))
         shift = top * slope
-        diag = jnp.exp2(diag * slope - shift)
-        total = jnp.sum(diag, axis=-1, keepdims=True)
         if start:
             past = jnp.exp2(past * slope - shift)
-            total = total + jnp.sum(past, axis=-1, keepdims=True)
-        inv = 1.0 / total
-        out = jnp.dot((diag * inv).astype(BF16), v_ref[start:end], preferred_element_type=F32)
-        if start:
-            out = out + jnp.dot((past * inv).astype(BF16), v_ref[:start], preferred_element_type=F32)
-        o_ref[start:end] = out.astype(BF16)
+            total = jnp.sum(past, axis=0, keepdims=True)
+            out = weigh(0, start, past)
+        for i, skip in enumerate(range(0, block, step)):
+            probs = jnp.exp2(near[i] * slope - shift[:, skip:])
+            total = update(total, skip, jnp.sum(probs, axis=0, keepdims=True), jnp.add)
+            out = update(out, skip, weigh(start + skip, start + skip + step, probs), jnp.add)
+        o_ref[start : start + block] = (out / total).astype(BF16).T
 
 
 def attention(qkv, heads, scale):
     seq_len = qkv.shape[0]
     spec = lambda first: pl.BlockSpec((seq_len, LANES), lambda h: (0, first + h))
     return pl.pallas_call(
-        functools.partial(attention_kernel, scale, 256),
+        functools.partial(attention_kernel, scale, 1024, 256),
         grid=(heads,),
         out_shape=jax.ShapeDtypeStruct((seq_len, heads * LANES), BF16),
         in_specs=[spec(0), spec(heads), spec(2 * heads)],
         out_specs=spec(0),
-        compiler_params=pltpu.CompilerParams(vmem_limit_bytes=50 << 20),
+        compiler_params=pltpu.CompilerParams(vmem_limit_bytes=60 << 20),
         cost_estimate=pl.CostEstimate(flops=2 * heads * seq_len * seq_len * LANES, bytes_accessed=8 << 20, transcendentals=heads * seq_len * seq_len // 2),
         name="attention",
     )(qkv, qkv, qkv)

time: 676 us -> 654 us (0.967)
  Pallas kernels: 527 us -> 508 us
    pallas_call x2, Pallas kernels: 49.8 us -> 30.6 us  [attention(): pl.pallas_call(functools.partial(attention_kernel, scale, 1024, 256), gri...]
where the time goes in v4:
time: 654 us
  Pallas kernels  508 us (78%)
  waiting for transfers between devices  73.9 us (11%)
  local copies, waits for them, and re-layouts  29.1 us (4%)
  matrix products  22.2 us (3%)
  between operations  13.4 us (2%)
  other arithmetic  6.96 us (1%)
    pallas_call x2, Pallas kernels, layer_tail(): pl.pallas_call(functools.partial(layer_kernel, chips, per_core, span, lay...  477 us
    all_gather x1, waiting for transfers between devices, local_forward(): gathered = lax.all_gather(normed, 'tp', axis=0, tiled=True)  73.9 us
    pallas_call x2, Pallas kernels, attention(): pl.pallas_call(functools.partial(attention_kernel, scale, 1024, 256), gri...  30.6 us
    dot_general x1, matrix products, local_forward(): qkv = jnp.dot(gathered, wq[0], preferred_element_type=F32).astype(BF16)  22.2 us
  transfers between devices with their start and end apart: 1, of which 1 were waited for; matrix products, arithmetic and copies ran while one was open for 4% of the time, Pallas kernels for 0%

profile of v4, /device:TPU:0, one launch (start us, length us, event | category | flops | bytes accessed | tf_op | source)
XLA Modules:
  0.0 653.6 jit_solution(2079407114288836231)
XLA Ops:
  6.5 0.0 all-gather.2.cloned.1.call-start
  6.5 1.7 convert_reduce_fusion
  8.2 1.8 multiply_reduce_fusion
  10.0 0.0 copy-done.7
  10.0 0.0 copy-done.6
  10.1 0.6 fusion.4
  10.7 1.6 add_convert_fusion
  12.3 0.0 all-gather.2.cloned.1.call-update
  12.3 10.3 %pad_slice_fusion = (bf16[1,2560,3,4,128]{1,4,3,2,0:T(8,128)(2,1)}, bf16[1,2560,3,4,128]{1,4,3,2,0:T(8,128)(2,1)}) fusion(bf16[2,2560,3,4,80]{1,4,3,2,0:T(8,128)(2,1)} %param.17), kind=kLoop, calls=%fused_computation | loop fusion | bytes 25559040 | tf_op jit(solution)/shard_map/slice | solution.py:406
  22.7 10.7 %copy.14.refs_10_ = bf16[2560,1536]{1,0:T(8,128)(2,1)} copy(bf16[2560,1536]{0,1:T(8,128)(2,1)} %bitcast.21) | data formatting | bytes 15728640 | tf_op jit(solution)/shard_map/squeeze | solution.py:406
  33.3 1.8 convert.1.refs_1_
  35.2 0.0 copy-done.8
  35.2 0.6 fusion.6
  35.8 0.4 copy-done.1
  36.2 2.7 pad_slice_fusion.2
  38.9 0.6 fusion
  39.6 0.6 fusion.2
  40.2 73.9 %all-gather.2.cloned.1.call-done = bf16[2048,2560]{1,0:T(8,128)(2,1)} async-done(((bf16[256,2560]{1,0:T(8,128)(2,1)}), bf16[2048,2560]{1,0:T(8,128)(2,1)}) %all-gather.2.cloned.1.call-update) | async-done | bytes 10485776 | tf_op jit(solution)/shard_map/all_gather | solution.py:399
  114.1 22.2 %convolution_convert_fusion.q_ref.k_ref.v_ref = bf16[2048,1536]{1,0:T(8,128)(2,1)} fusion(bf16[2048,2560]{1,0:T(8,128)(2,1)} %all-gather.2.cloned.1.call-done, bf16[2560,1536]{0,1:T(8,128)(2,1)} %bitcast.23), kind=kOutput, calls=%fused_computation.2 | convolution fusion | flops 16109273088 | bytes 24641536 | tf_op jit(solution)/shard_map/dot_general | solution.py:400
  136.3 15.3 %attention.2 = bf16[2048,512]{1,0:T(8,128)(2,1)} custom-call(bf16[2048,1536]{1,0:T(8,128)(2,1)} %convolution_convert_fusion.q_ref.k_ref.v_ref, bf16[2048,1536]{1,0:T(8,128)(2,1)} %convolution_convert_fusion.q_ref.k_ref.v_ref, bf16[2048,1536]{1,0:T(8,128)(2,1)} %convolution_convert_fusion.q_ref.k_ref.v_ref), custom_call_target="tpu_custom_call" | custom-call | flops 4294967296 | bytes 8388608 | tf_op jit(solution)/shard_map/attention/pallas_call | solution.py:375
  151.7 265.8 %layer0.1 = (bf16[4,2,16,16,1536]{4,3,2,1,0:T(8,128)(2,1)}, f32[16,16,2560]{2,1,0:T(8,128)}) custom-call(bf16[4,2,16,16,512]{4,3,2,1,0:T(8,128)(2,1)} %bitcast.26, f32[16,16,2560]{2,1,0:T(8,128)} %convert.1.refs_1_, bf16[512,2560]{1,0:T(8,128)(2,1)} %bitcast.25, bf16[2,2560,1280]{2,1,0:T(8,128)(2,1)} %refs_3_.3, bf16[2,1280,2560]{2,1,0:T(8,128)(2,1)} %refs_4_.3, ...), custom_call_target="tpu_custom_call" | custom-call | flops 48318382080 | bytes 41943040 | tf_op jit(solution)/shard_map/layer0/pallas_call | solution.py:314
  417.4 15.3 %attention.3 = bf16[2048,512]{1,0:T(8,128)(2,1)} custom-call(bf16[2048,1536]{1,0:T(8,128)(2,1)} %bitcast.18, bf16[2048,1536]{1,0:T(8,128)(2,1)} %bitcast.19, bf16[2048,1536]{1,0:T(8,128)(2,1)} %bitcast.20), custom_call_target="tpu_custom_call" | custom-call | flops 4294967296 | bytes 8388608 | tf_op jit(solution)/shard_map/attention/pallas_call | solution.py:375
  432.8 211.5 %layer1.1 = bf16[16,16,2560]{2,1,0:T(8,128)(2,1)} custom-call(bf16[4,2,16,16,512]{4,3,2,1,0:T(8,128)(2,1)} %bitcast.27, f32[16,16,2560]{2,1,0:T(8,128)} %get-tuple-element.8.refs_1_, bf16[512,2560]{1,0:T(8,128)(2,1)} %bitcast.24, bf16[2,2560,1280]{2,1,0:T(8,128)(2,1)} %refs_3_.3, bf16[2,1280,2560]{2,1,0:T(8,128)(2,1)} %refs_4_.3, ...), custom_call_target="tpu_custom_call" | custom-call | flops 32212254720 | bytes 41943040 | tf_op jit(solution)/shard_map/layer1/pallas_call | solution.py:314
  644.3 2.5 copy.16
  (16 shorter events, 0.0 us)
Async XLA Ops:
  6.5 4.2 copy-start
  6.5 3.5 copy-start.7
  6.5 3.5 copy-start.6
  6.5 107.6 %all-gather.2.cloned.1.call-start = ((), (), s32[]{:S(2)}) async-start(), calls=%async_computation | async-start | bytes 11796480 | tf_op jit(solution)/shard_map/all_gather | solution.py:399
  33.3 1.9 copy-start.8
  33.3 2.9 copy-start.1
  36.2 2.7 copy-start.2
  36.2 2.7 copy-start.3
  36.2 3.4 copy-start.4
  36.2 3.4 copy-start.5
Sparse Core Ops, SparseCore 0:
  12.5 101.6 all-gather.1

commit v5 on v4

--- a/solution.py
+++ b/solution.py
@@ -14,6 +14,7 @@
 AHEAD = 4
 HOP = 4
 MESH = pl.DeviceIdType.MESH
+LAST = (((1,), (1,)), ((), ()))
 
 
 def layer_norm(resid, gain, shift):
@@ -35,6 +36,155 @@
 
 def chunk_place(j, chips):
     return owner_of(j % chips, chips), j // chips
+
+
+def padded_heads(src, dst):
+    heads, head_dim = src.shape[0], src.shape[1]
+    return [(src.at[h], dst.at[pl.ds(h * LANES, head_dim)]) for h in range(heads)]
+
+
+def clear_pads(ref, head_dim):
+    for start in range(0, ref.shape[0], LANES):
+        ref[start + head_dim : start + LANES] = jnp.zeros((LANES - head_dim, ref.shape[1]), ref.dtype)
+
+
+def head_kernel(chips, per_core, x_ref, gain, shift, w_qkv_hbm, qkv_hbm, resid, normed, w_qkv, qkv_buf, qkv_s, copy_s,
+                norm_r, left_s, right_s, mate_s, mate_r):
+    n_chunks = chips * per_core
+    far = chips - 1
+    heads, head_dim = w_qkv_hbm.shape[2], w_qkv_hbm.shape[3]
+    group = lax.axis_index("dp")
+    me = lax.axis_index("tp")
+    z, core = me // 2, me % 2
+    mate = (group, z * 2 + (1 - core))
+    left = (group, jnp.maximum(me - 2, 0))
+    right = (group, jnp.minimum(me + 2, 2 * chips - 1))
+    has_left, has_right = z > 0, z < far
+
+    loads = []
+    for part in range(3):
+        loads += padded_heads(w_qkv_hbm.at[0, part], w_qkv.at[pl.ds(part * heads * LANES, heads * LANES)])
+    loads = [pltpu.make_async_copy(src, dst, copy_s.at[i]) for i, (src, dst) in enumerate(loads)]
+    for load in loads:
+        load.start()
+    clear_pads(w_qkv, head_dim)
+
+    def remote(rows, send, recv, device):
+        return pltpu.make_async_remote_copy(src_ref=rows, dst_ref=rows, send_sem=send, recv_sem=recv, device_id=device, device_id_type=MESH)
+
+    barrier = pltpu.get_barrier_semaphore()
+    pl.semaphore_signal(barrier, inc=1, device_id=mate, device_id_type=MESH)
+
+    @pl.when(has_left)
+    def _():
+        pl.semaphore_signal(barrier, inc=1, device_id=left, device_id_type=MESH)
+
+    @pl.when(has_right)
+    def _():
+        pl.semaphore_signal(barrier, inc=1, device_id=right, device_id_type=MESH)
+
+    pl.semaphore_wait(barrier, 1 + has_left.astype(jnp.int32) + has_right.astype(jnp.int32))
+
+    def to_left(j, rows):
+        return remote(rows, left_s.at[j], norm_r.at[j], left)
+
+    def to_right(j, rows):
+        return remote(rows, right_s.at[j], norm_r.at[j], right)
+
+    def to_mate(j, rows):
+        return remote(rows, mate_s.at[j], mate_r.at[j], mate)
+
+    def own_norm(j, owner, place):
+        total = x_ref[place].astype(F32)
+        resid[place] = total
+        rows = normed.at[owner, core, place]
+        rows[...] = layer_norm(total, gain[...], shift[...])
+        pl.when(has_left)(lambda: to_left(j, rows).start())
+        pl.when(has_right)(lambda: to_right(j, rows).start())
+        to_mate(j, rows).start()
+
+    def pass_norm(j, owner, place):
+        rows = normed.at[owner, core, place]
+        to_left(j, rows).wait_recv()
+        pl.when((z < owner) & has_left)(lambda: to_left(j, rows).start())
+        pl.when((z > owner) & has_right)(lambda: to_right(j, rows).start())
+        to_mate(j, rows).start()
+
+    def qkv_copy(place):
+        return pltpu.make_async_copy(qkv_buf.at[place % 2], qkv_hbm.at[:, :, place], qkv_s.at[place % 2])
+
+    def project_qkv(j):
+        place = j // chips
+
+        @pl.when(j == 0)
+        def _():
+            for load in loads:
+                load.wait()
+
+        pl.when(place >= 2)(lambda: qkv_copy(place - 2).wait())
+        for turn in range(chips):
+            to_mate(j + turn, normed.at[owner_of(turn, chips), 1 - core, place]).wait_recv()
+        rows = normed[:, :, place].reshape(chips * 2 * CHUNK, normed.shape[-1])
+        for start, width in col_tiles(w_qkv.shape[0]):
+            tile = lax.dot_general(rows, w_qkv[start : start + width], LAST, preferred_element_type=F32)
+            qkv_buf[place % 2, :, :, :, start : start + width] = tile.astype(BF16).reshape(chips, 2, CHUNK, width)
+        qkv_copy(place).start()
+
+    def at_distance(j, distance, step):
+        inside = (j >= 0) & (j < n_chunks)
+        safe = jnp.clip(j, 0, n_chunks - 1)
+        owner, place = chunk_place(safe, chips)
+        pl.when(inside & (jnp.abs(z - owner) == distance))(lambda: step(safe, owner, place))
+
+    span = HOP * far + chips
+
+    def tick(t, carry):
+        for distance in range(chips):
+            at_distance(t - HOP * distance, distance, pass_norm if distance else own_norm)
+        j = t - span
+        pl.when((j >= 0) & (j % chips == 0))(lambda: project_qkv(jnp.clip(j, 0, n_chunks - chips)))
+        return carry
+
+    lax.fori_loop(0, span + n_chunks - chips + 1, tick, 0)
+
+    def drain(j, carry):
+        owner, place = chunk_place(j, chips)
+        rows = normed.at[owner, core, place]
+        pl.when((z <= owner) & has_left)(lambda: to_left(j, rows).wait_send())
+        pl.when((z >= owner) & has_right)(lambda: to_right(j, rows).wait_send())
+        to_mate(j, rows).wait_send()
+        return carry
+
+    lax.fori_loop(0, n_chunks, drain, 0)
+    qkv_copy(per_core - 2).wait()
+    qkv_copy(per_core - 1).wait()
+
+
+def layer_head(chips, call_id, x, gain, shift, w_qkv):
+    own, width = x.shape
+    per_core = own // CHUNK
+    n_chunks = chips * per_core
+    width2 = 3 * w_qkv.shape[2] * LANES
+    blocks = (chips, 2, per_core, CHUNK)
+    any_spec = pl.BlockSpec(memory_space=pl.ANY)
+    vmem = pl.BlockSpec(memory_space=pltpu.VMEM)
+    qkv, resid = pl.pallas_call(
+        functools.partial(head_kernel, chips, per_core),
+        out_shape=(jax.ShapeDtypeStruct((*blocks, width2), BF16), jax.ShapeDtypeStruct((per_core, CHUNK, width), F32)),
+        in_specs=[vmem, vmem, vmem, any_spec],
+        out_specs=(any_spec, vmem),
+        scratch_shapes=[
+            pltpu.VMEM((*blocks, width), BF16),
+            pltpu.VMEM((width2, width), BF16),
+            pltpu.VMEM((2, chips, 2, CHUNK, width2), BF16),
+            pltpu.SemaphoreType.DMA((2,)),
+            pltpu.SemaphoreType.DMA((3 * w_qkv.shape[2],)),
+        ] + [pltpu.SemaphoreType.DMA((n_chunks,))] * 5,
+        compiler_params=pltpu.CompilerParams(collective_id=call_id, has_side_effects=True, vmem_limit_bytes=67043328),
+        cost_estimate=pl.CostEstimate(flops=2 * 2 * chips * own * width * width2, bytes_accessed=20 << 20, transcendentals=0),
+        name="head",
+    )(x.reshape(per_core, CHUNK, width), gain[None], shift[None], w_qkv)
+    return qkv.reshape(2 * chips * own, width2), resid.reshape(own, width)
 
 
 class Stage:
@@ -76,12 +226,20 @@
     right = (group, jnp.minimum(me + 2, 2 * chips - 1))
     has_left, has_right = z > 0, z < far
 
-    loads = [(x_hbm, x_ref), (w_out_hbm, w_out), (resid_hbm, resid), (w_up_hbm.at[layer], w_up), (w_down_hbm.at[layer], w_down)]
+    heads = w_out_hbm.shape[1]
+    loads = [(x_hbm, x_ref), (resid_hbm, resid)] + padded_heads(w_out_hbm.at[layer], w_out)
+    n_first = len(loads)
+    loads += [(w_up_hbm.at[layer], w_up), (w_down_hbm.at[layer], w_down)]
+    n_mlp = len(loads)
     if not final:
-        loads.append((w_qkv_hbm, w_qkv))
+        for part in range(3):
+            loads += padded_heads(w_qkv_hbm.at[layer + 1, part], w_qkv.at[pl.ds(part * heads * LANES, heads * LANES)])
     loads = [pltpu.make_async_copy(src, dst, copy_s.at[i]) for i, (src, dst) in enumerate(loads)]
     for load in loads:
         load.start()
+    clear_pads(w_out, w_out_hbm.shape[2])
+    if not final:
+        clear_pads(w_qkv, w_out_hbm.shape[2])
 
     def remote(src, dst, send, recv, device):
         return pltpu.make_async_remote_copy(src_ref=src, dst_ref=dst, send_sem=send, recv_sem=recv, device_id=device, device_id_type=MESH)
@@ -98,7 +256,7 @@
         pl.semaphore_signal(barrier, inc=1, device_id=right, device_id_type=MESH)
 
     pl.semaphore_wait(barrier, 1 + has_left.astype(jnp.int32) + has_right.astype(jnp.int32))
-    for load in loads[:3]:
+    for load in loads[:n_first]:
         load.wait()
 
     def store_part(s, j, rows, w_ref):
@@ -206,8 +364,8 @@
     def mlp(j):
         @pl.when(j == 0)
         def _():
-            loads[3].wait()
-            loads[4].wait()
+            for load in loads[n_first:n_mlp]:
+                load.wait()
 
         rows = normed_rows(stage_a, j)
         for start, width in col_tiles(w_up.shape[1]):
@@ -221,11 +379,16 @@
 
     def project_qkv(j):
         place = j // chips
-        pl.when(j == 0)(lambda: loads[5].wait())
+
+        @pl.when(j == 0)
+        def _():
+            for load in loads[n_mlp:]:
+                load.wait()
+
         pl.when(place >= 2)(lambda: qkv_copy(place - 2).wait())
         rows = normed_rows(stage_b, j)
-        for start, width in col_tiles(w_qkv.shape[1]):
-            tile = jnp.dot(rows, w_qkv[:, start : start + width], preferred_element_type=F32)
+        for start, width in col_tiles(w_qkv.shape[0]):
+            tile = lax.dot_general(rows, w_qkv[start : start + width], LAST, preferred_element_type=F32)
             qkv_buf[place % 2, :, :, :, start : start + width] = tile.astype(BF16).reshape(chips, 2, CHUNK, width)
         qkv_copy(place).start()
 
@@ -295,7 +458,7 @@
         pltpu.VMEM((mid, width), BF16),
         pltpu.VMEM((chips * 2 * CHUNK, mid), BF16),
         pltpu.VMEM((CHUNK, width), F32),
-        pltpu.SemaphoreType.DMA((6,)),
+        pltpu.SemaphoreType.DMA((4 + 4 * w_out.shape[1],)),
     ] + slots + norm_slots + sems * 10
     flops = 2 * seq_len * width * (depth + 2 * mid)
     if final:
@@ -303,13 +466,13 @@
         out_specs = vmem
         scratch += slots + sems * 5 + [pltpu.VMEM((per_core, CHUNK, width), F32)]
     else:
-        width2 = w_qkv.shape[1]
+        width2 = 3 * w_qkv.shape[2] * LANES
         operands += [w_qkv, norm_b[0][None], norm_b[1][None]]
         in_specs += [any_spec, vmem, vmem]
         out_shape = (jax.ShapeDtypeStruct((*blocks, width2), BF16), jax.ShapeDtypeStruct((per_core, CHUNK, width), F32))
         out_specs = (any_spec, vmem)
         scratch += slots + norm_slots + sems * 10
-        scratch += [pltpu.VMEM((width, width2), BF16), pltpu.VMEM((2, chips, 2, CHUNK, width2), BF16), pltpu.SemaphoreType.DMA((2,))]
+        scratch += [pltpu.VMEM((width2, width), BF16), pltpu.VMEM((2, chips, 2, CHUNK, width2), BF16), pltpu.SemaphoreType.DMA((2,))]
         flops += 2 * seq_len * width * width2
     result = pl.pallas_call(
         functools.partial(layer_kernel, chips, per_core, span, layer, final),
@@ -391,19 +554,14 @@
     def local_forward(x_local, ln1_gain, ln1_bias, ln2_gain, ln2_bias, w_qkv, w_out, b_out, w_up, b_up, w_down, b_down):
         layers, width, _, heads, head_dim = w_qkv.shape
         scale = 1.0 / math.sqrt(head_dim)
-        pad = LANES - head_dim
-        wq = jnp.pad(w_qkv, ((0, 0), (0, 0), (0, 0), (0, 0), (0, pad))).reshape(layers, width, 3 * heads * LANES)
-        wo = jnp.pad(w_out, ((0, 0), (0, 0), (0, pad), (0, 0))).reshape(layers, heads * LANES, width)
-        resid = x_local[0].astype(F32)
-        normed = layer_norm(resid, ln1_gain[0], ln1_bias[0])
-        gathered = lax.all_gather(normed, "tp", axis=0, tiled=True)
-        qkv = jnp.dot(gathered, wq[0], preferred_element_type=F32).astype(BF16)
+        w_qkv = jnp.transpose(w_qkv, (0, 2, 3, 4, 1))
+        qkv, resid = layer_head(chips, layers, x_local[0], ln1_gain[0], ln1_bias[0], w_qkv)
         for layer in range(layers):
             heads_out = attention(qkv, heads, scale)
-            args = (chips, layer, heads_out, resid, wo[layer], w_up, w_down, b_out[layer],
+            args = (chips, layer, heads_out, resid, w_out, w_up, w_down, b_out[layer],
                     (ln2_gain[layer], ln2_bias[layer]), b_up[layer], b_down[layer])
             if layer + 1 < layers:
-                qkv, resid = layer_tail(*args, (ln1_gain[layer + 1], ln1_bias[layer + 1]), wq[layer + 1])
+                qkv, resid = layer_tail(*args, (ln1_gain[layer + 1], ln1_bias[layer + 1]), w_qkv)
             else:
                 out = layer_tail(*args)
         return out[None]

time: 654 us -> 628 us (0.960)
  Pallas kernels: 508 us -> 619 us
  waiting for transfers between devices: 73.9 us -> 0 us
  matrix products: 22.2 us -> 0 us
  local copies, waits for them, and re-layouts: 29.1 us -> 8.16 us
  between operations: 13.4 us -> 0.03 us
  other arithmetic: 6.96 us -> 0 us
    pallas_call x0 -> x1, Pallas kernels: none -> 106 us  [layer_head(): pl.pallas_call(functools.partial(head_kernel, chips, per_core), out_shape...]
    all_gather x1 -> x0, waiting for transfers between devices: 73.9 us -> none  [local_forward(): gathered = lax.all_gather(normed, 'tp', axis=0, tiled=True)]
    dot_general x1 -> x0, matrix products: 22.2 us -> none  [local_forward(): qkv = jnp.dot(gathered, wq[0], preferred_element_type=F32).astype(BF16)]
    slice x2 -> x0, local copies, waits for them, and re-layouts: 13 us -> none  [the longest x1 10.3 us: local_forward(): wq[layer + 1]]
    squeeze x1 -> x0, local copies, waits for them, and re-layouts: 10.7 us -> none  [local_forward(): wq[layer + 1]]
  transfers between devices with their start and end apart: 1 -> 0, of which waited for: 1 -> 0; matrix products, arithmetic and copies ran while one was open for 4% -> 0% of each run, Pallas kernels for 0% -> 0%
where the time goes in v5:
time: 628 us; the launch traced here: 627 us
  Pallas kernels  619 us (99%)
  local copies, waits for them, and re-layouts  8.16 us (1%)
    pallas_call x2, Pallas kernels, layer_tail(): pl.pallas_call(functools.partial(layer_kernel, chips, per_core, span, lay...  482 us
    pallas_call x1, Pallas kernels, layer_head(): pl.pallas_call(functools.partial(head_kernel, chips, per_core), out_shape...  106 us
    pallas_call x2, Pallas kernels, attention(): pl.pallas_call(functools.partial(attention_kernel, scale, 1024, 256), gri...  30.6 us

profile of v5, /device:TPU:0, one launch (start us, length us, event | category | flops | bytes accessed | tf_op | source)
XLA Modules:
  0.0 627.0 jit_solution(5356421182559414898)
XLA Ops:
  0.0 1.4 fusion.6
  1.4 1.4 fusion.4
  2.8 1.4 fusion.2
  4.3 1.4 fusion
  5.7 105.8 %head.1 = (bf16[4,2,16,16,1536]{4,3,2,1,0:T(8,128)(2,1)}, f32[16,16,2560]{2,1,0:T(8,128)}) custom-call(bf16[16,16,2560]{2,1,0:T(8,128)(2,1)} %bitcast.18, f32[1,2560]{1,0:T(1,128)} %get-tuple-element.27.gain, f32[1,2560]{1,0:T(1,128)} %get-tuple-element.22.shift, bf16[2,3,4,80,2560]{4,3,2,1,0:T(8,128)(2,1)} %bitcast.16), custom_call_target="tpu_custom_call" | custom-call | flops 16106127360 | bytes 20971520 | tf_op jit(solution)/shard_map/head/pallas_call | solution.py:171
  111.5 15.3 %attention.2 = bf16[2048,512]{1,0:T(8,128)(2,1)} custom-call(bf16[2048,1536]{1,0:T(8,128)(2,1)} %bitcast.10, bf16[2048,1536]{1,0:T(8,128)(2,1)} %bitcast.11, bf16[2048,1536]{1,0:T(8,128)(2,1)} %bitcast.12), custom_call_target="tpu_custom_call" | custom-call | flops 4294967296 | bytes 8388608 | tf_op jit(solution)/shard_map/attention/pallas_call | solution.py:538
  126.8 270.6 %layer0.1 = (bf16[4,2,16,16,1536]{4,3,2,1,0:T(8,128)(2,1)}, f32[16,16,2560]{2,1,0:T(8,128)}) custom-call(bf16[4,2,16,16,512]{4,3,2,1,0:T(8,128)(2,1)} %bitcast.13, f32[16,16,2560]{2,1,0:T(8,128)} %get-tuple-element.10.refs_1_, bf16[2,4,80,2560]{3,2,1,0:T(8,128)(2,1)} %refs_2_.3, bf16[2,2560,1280]{2,1,0:T(8,128)(2,1)} %refs_3_.3, ...), custom_call_target="tpu_custom_call" | custom-call | flops 48318382080 | bytes 41943040 | tf_op jit(solution)/shard_map/layer0/pallas_call | solution.py:477
  397.4 15.3 %attention.3 = bf16[2048,512]{1,0:T(8,128)(2,1)} custom-call(bf16[2048,1536]{1,0:T(8,128)(2,1)} %bitcast.7, bf16[2048,1536]{1,0:T(8,128)(2,1)} %bitcast.8, bf16[2048,1536]{1,0:T(8,128)(2,1)} %bitcast.9), custom_call_target="tpu_custom_call" | custom-call | flops 4294967296 | bytes 8388608 | tf_op jit(solution)/shard_map/attention/pallas_call | solution.py:538
  412.8 211.8 %layer1.1 = bf16[16,16,2560]{2,1,0:T(8,128)(2,1)} custom-call(bf16[4,2,16,16,512]{4,3,2,1,0:T(8,128)(2,1)} %bitcast.14, f32[16,16,2560]{2,1,0:T(8,128)} %get-tuple-element.12.refs_1_, bf16[2,4,80,2560]{3,2,1,0:T(8,128)(2,1)} %refs_2_.3, bf16[2,2560,1280]{2,1,0:T(8,128)(2,1)} %refs_3_.3, bf16[2,1280,2560]{2,1,0:T(8,128)(2,1)} %refs_4_.3, ...), custom_call_target="tpu_custom_call" | custom-call | flops 32212254720 | bytes 41943040 | tf_op jit(solution)/shard_map/layer1/pallas_call | solution.py:477
  624.5 2.5 copy.14

commit v6 on v5

--- a/solution.py
+++ b/solution.py
@@ -36,6 +36,10 @@
 
 def chunk_place(j, chips):
     return owner_of(j % chips, chips), j // chips
+
+
+def row_of(ref, row):
+    return ref[row : row + 1]
 
 
 def padded_heads(src, dst):
@@ -98,7 +102,7 @@
         total = x_ref[place].astype(F32)
         resid[place] = total
         rows = normed.at[owner, core, place]
-        rows[...] = layer_norm(total, gain[...], shift[...])
+        rows[...] = layer_norm(total, row_of(gain, 0), row_of(shift, 0))
         pl.when(has_left)(lambda: to_left(j, rows).start())
         pl.when(has_right)(lambda: to_right(j, rows).start())
         to_mate(j, rows).start()
@@ -183,7 +187,7 @@
         compiler_params=pltpu.CompilerParams(collective_id=call_id, has_side_effects=True, vmem_limit_bytes=67043328),
         cost_estimate=pl.CostEstimate(flops=2 * 2 * chips * own * width * width2, bytes_accessed=20 << 20, transcendentals=0),
         name="head",
-    )(x.reshape(per_core, CHUNK, width), gain[None], shift[None], w_qkv)
+    )(x.reshape(per_core, CHUNK, width), gain, shift, w_qkv)
     return qkv.reshape(2 * chips * own, width2), resid.reshape(own, width)
 
 
@@ -207,12 +211,12 @@
     else:
         w_qkv_hbm, gain_b, shift_b, qkv_hbm, resid = take(5)
     x_ref, w_out, w_up, w_down, hidden, acc_ref, copy_s = take(7)
-    stage_a = Stage(0, take(5), take(10), bias_a, gain_a, shift_a)
+    stage_a = Stage(0, take(5), take(10), (bias_a, layer), (gain_a, layer), (shift_a, layer))
     if final:
-        stage_b = Stage(span, take(4), take(5), bias_b)
+        stage_b = Stage(span, take(4), take(5), (bias_b, layer))
         (resid,) = take(1)
     else:
-        stage_b = Stage(span, take(5), take(10), bias_b, gain_b, shift_b)
+        stage_b = Stage(span, take(5), take(10), (bias_b, layer), (gain_b, layer + 1), (shift_b, layer + 1))
         w_qkv, qkv_buf, qkv_s = take(3)
     n_chunks = chips * per_core
     far = chips - 1
@@ -319,13 +323,13 @@
             remote(s.inc2.at[at], s.inc2.at[at], s.sum_s.at[n], s.inc2_r.at[n], right).wait_recv()
             acc_ref[...] += s.inc2[at].astype(F32)
 
-        total = resid[place] + (acc_ref[...] + s.bias[...])
+        total = resid[place] + (acc_ref[...] + row_of(*s.bias))
         if s.final:
             y_ref[place] = total.astype(BF16)
             return
         resid[place] = total
         rows = s.normed.at[owner, core, at]
-        rows[...] = layer_norm(total, s.gain[...], s.shift[...])
+        rows[...] = layer_norm(total, row_of(*s.gain), row_of(*s.shift))
         pl.when(has_left)(lambda: send_left(s, n, rows))
         pl.when(has_right)(lambda: send_right(s, n, rows))
         remote(rows, rows, s.mate_s.at[n], s.mate_r.at[n], mate).start()
@@ -370,7 +374,7 @@
         rows = normed_rows(stage_a, j)
         for start, width in col_tiles(w_up.shape[1]):
             tile = jnp.dot(rows, w_up[:, start : start + width], preferred_element_type=F32)
-            hidden[:, start : start + width] = jax.nn.gelu(tile + b_up[:, start : start + width], approximate=True).astype(BF16)
+            hidden[:, start : start + width] = jax.nn.gelu(tile + b_up[layer : layer + 1, start : start + width], approximate=True).astype(BF16)
         pl.when(j >= span)(lambda: release(stage_b, j - span))
         store_part(stage_b, j, hidden[...], w_down)
 
@@ -441,7 +445,7 @@
     any_spec = pl.BlockSpec(memory_space=pl.ANY)
     vmem = pl.BlockSpec(memory_space=pltpu.VMEM)
     operands = [x.reshape(*blocks, depth), resid.reshape(per_core, CHUNK, width), w_out, w_up, w_down,
-                bias_a[None], norm_a[0][None], norm_a[1][None], b_up[None], bias_b[None]]
+                bias_a, *norm_a, b_up, bias_b]
     in_specs = [any_spec] * 5 + [vmem] * 5
     sems = [pltpu.SemaphoreType.DMA((span,))]
     slots = [
@@ -467,7 +471,7 @@
         scratch += slots + sems * 5 + [pltpu.VMEM((per_core, CHUNK, width), F32)]
     else:
         width2 = 3 * w_qkv.shape[2] * LANES
-        operands += [w_qkv, norm_b[0][None], norm_b[1][None]]
+        operands += [w_qkv, *norm_b]
         in_specs += [any_spec, vmem, vmem]
         out_shape = (jax.ShapeDtypeStruct((*blocks, width2), BF16), jax.ShapeDtypeStruct((per_core, CHUNK, width), F32))
         out_specs = (any_spec, vmem)
@@ -555,13 +559,13 @@
         layers, width, _, heads, head_dim = w_qkv.shape
         scale = 1.0 / math.sqrt(head_dim)
         w_qkv = jnp.transpose(w_qkv, (0, 2, 3, 4, 1))
-        qkv, resid = layer_head(chips, layers, x_local[0], ln1_gain[0], ln1_bias[0], w_qkv)
+        qkv, resid = layer_head(chips, layers, x_local[0], ln1_gain, ln1_bias, w_qkv)
         for layer in range(layers):
             heads_out = attention(qkv, heads, scale)
-            args = (chips, layer, heads_out, resid, w_out, w_up, w_down, b_out[layer],
-                    (ln2_gain[layer], ln2_bias[layer]), b_up[layer], b_down[layer])
+            args = (chips, layer, heads_out, resid, w_out, w_up, w_down, b_out,
+                    (ln2_gain, ln2_bias), b_up, b_down)
             if layer + 1 < layers:
-                qkv, resid = layer_tail(*args, (ln1_gain[layer + 1], ln1_bias[layer + 1]), w_qkv)
+                qkv, resid = layer_tail(*args, (ln1_gain, ln1_bias), w_qkv)
             else:
                 out = layer_tail(*args)
         return out[None]

time: 628 us -> 622 us (level)
  no operation moved by 1% of the time
where the time goes in v6:
time: 622 us; the launch traced here: 621 us
  Pallas kernels  619 us (100%)
    pallas_call x2, Pallas kernels, layer_tail(): pl.pallas_call(functools.partial(layer_kernel, chips, per_core, span, lay...  482 us
    pallas_call x1, Pallas kernels, layer_head(): pl.pallas_call(functools.partial(head_kernel, chips, per_core), out_shape...  106 us
    pallas_call x2, Pallas kernels, attention(): pl.pallas_call(functools.partial(attention_kernel, scale, 1024, 256), gri...  30.7 us

profile of v6, /device:TPU:0, one launch (start us, length us, event | category | flops | bytes accessed | tf_op | source)
XLA Modules:
  0.0 621.4 jit_solution(12696318179414281652)
XLA Ops:
  0.0 105.8 %head.1 = (bf16[4,2,16,16,1536]{4,3,2,1,0:T(8,128)(2,1)}, f32[16,16,2560]{2,1,0:T(8,128)}) custom-call(bf16[16,16,2560]{2,1,0:T(8,128)(2,1)} %bitcast.18, f32[2,2560]{1,0:T(2,128)} %refs_11_.1, f32[2,2560]{1,0:T(2,128)} %refs_12_.1, bf16[2,3,4,80,2560]{4,3,2,1,0:T(8,128)(2,1)} %bitcast.16), custom_call_target="tpu_custom_call" | custom-call | flops 16106127360 | bytes 20971520 | tf_op jit(solution)/shard_map/head/pallas_call | solution.py:175
  105.8 15.3 %attention.2 = bf16[2048,512]{1,0:T(8,128)(2,1)} custom-call(bf16[2048,1536]{1,0:T(8,128)(2,1)} %bitcast.10, bf16[2048,1536]{1,0:T(8,128)(2,1)} %bitcast.11, bf16[2048,1536]{1,0:T(8,128)(2,1)} %bitcast.12), custom_call_target="tpu_custom_call" | custom-call | flops 4294967296 | bytes 8388608 | tf_op jit(solution)/shard_map/attention/pallas_call | solution.py:542
  121.1 270.6 %layer0.1 = (bf16[4,2,16,16,1536]{4,3,2,1,0:T(8,128)(2,1)}, f32[16,16,2560]{2,1,0:T(8,128)}) custom-call(bf16[4,2,16,16,512]{4,3,2,1,0:T(8,128)(2,1)} %bitcast.13, f32[16,16,2560]{2,1,0:T(8,128)} %get-tuple-element.10.refs_1_, bf16[2,4,80,2560]{3,2,1,0:T(8,128)(2,1)} %refs_2_.3, bf16[2,2560,1280]{2,1,0:T(8,128)(2,1)} %refs_3_.3, ...), custom_call_target="tpu_custom_call" | custom-call | flops 48318382080 | bytes 41943040 | tf_op jit(solution)/shard_map/layer0/pallas_call | solution.py:481
  391.7 15.3 %attention.3 = bf16[2048,512]{1,0:T(8,128)(2,1)} custom-call(bf16[2048,1536]{1,0:T(8,128)(2,1)} %bitcast.7, bf16[2048,1536]{1,0:T(8,128)(2,1)} %bitcast.8, bf16[2048,1536]{1,0:T(8,128)(2,1)} %bitcast.9), custom_call_target="tpu_custom_call" | custom-call | flops 4294967296 | bytes 8388608 | tf_op jit(solution)/shard_map/attention/pallas_call | solution.py:542
  407.1 211.8 %layer1.1 = bf16[16,16,2560]{2,1,0:T(8,128)(2,1)} custom-call(bf16[4,2,16,16,512]{4,3,2,1,0:T(8,128)(2,1)} %bitcast.14, f32[16,16,2560]{2,1,0:T(8,128)} %get-tuple-element.12.refs_1_, bf16[2,4,80,2560]{3,2,1,0:T(8,128)(2,1)} %refs_2_.3, bf16[2,2560,1280]{2,1,0:T(8,128)(2,1)} %refs_3_.3, bf16[2,1280,2560]{2,1,0:T(8,128)(2,1)} %refs_4_.3, f32[2,2560]{1,0:T(2,128)} %refs_5_.3, ...), custom_call_target="tpu_custom_call" | custom-call | flops 32212254720 | bytes 41943040 | tf_op jit(solution)/shard_map/layer1/pallas_call | solution.py:481
  618.9 2.5 copy.14
